TPU v7x, 128 devices: a whole 4x4x4 slice. The times are simulated.
128 devices in a mesh: gen: 16 (over x, z_hi, core), tp: 8 (over y, z_lo).
Axes of the slice: x: 4, y: 4, z: 4 (z_hi: 2, z_lo: 2; z = z_hi * 2 + z_lo), core: 2. Of those that a mesh axis runs over, the one named last changes fastest.
Arguments:
- hidden_in: bfloat16 [4, 32, 8192], P(None, 'gen'), may hold values from -6 to 6
- norm_gain: bfloat16 [8192], replicated, may hold values from 0.099609375 to 1.8984375
- w_query: bfloat16 [8192, 4096], P(('gen', 'tp')), may hold values from -0.0625 to 0.0625
- key_weight_matrix: bfloat16 [8192, 1024], P(('gen', 'tp')), may hold values from -0.0625 to 0.0625
- value_weight_matrix: bfloat16 [8192, 1024], P(('gen', 'tp')), may hold values from -0.0625 to 0.0625
- bias_query: bfloat16 [4096], P('tp'), may hold values from -3 to 3
- key_bias_vector: bfloat16 [1024], P('tp'), may hold values from -3 to 3
- value_bias_vector: bfloat16 [1024], P('tp'), may hold values from -3 to 3
- w_out: bfloat16 [4096, 8192], P(None, ('gen', 'tp')), may hold values from -0.09375 to 0.09375
- key_cache: bfloat16 [32, 8, 16384, 128], P('gen', 'tp'), may hold values from -400 to 400
- value_cache: bfloat16 [32, 8, 16384, 128], P('gen', 'tp'), may hold values from -16 to 16
- lengths: int32 [32], P('gen'), may hold values from 1 to 16384
- finished: int32 [32], P('gen'), may hold values 0 or 1
Outputs:
- layer_out: bfloat16 [4, 32, 8192], P(None, 'gen')
All inputs are finite; a program needn't handle non-finite values. No bound on the sum of `finished` on one device may be relied on, other than what follows from the above.
Results may differ from a plain program's by a relative error of at most 0.012.
Values may be sent and summed in bfloat16 or wider, within the bound.
A program may use at most 128 MiB of HBM per device.

v0:
```python
import math

import jax
import jax.numpy as jnp
from jax import lax
from jax.sharding import PartitionSpec as P

norm_eps = 1e-06
rope_base = 1000000.0
masked_score = -1e30


def sent_together(arrays, axis, dim, along):
    widths = [a.shape[along] for a in arrays]
    both = jnp.concatenate(arrays, axis=along)
    filled = lax.all_gather(both, axis, axis=dim, tiled=True)
    return tuple(jnp.split(filled, [sum(widths[:k]) for k in range(1, len(widths))], axis=along))


def from_everyone(array, axis):
    copies = jnp.broadcast_to(array, (lax.axis_size(axis), *array.shape))
    return lax.all_to_all(copies, axis, split_axis=0, concat_axis=0, tiled=True)


def of_everyone(array, axis):
    return from_everyone(array, axis).astype(jnp.float32).sum(axis=0)


def apply_rotation(values, token_positions):
    half_dim = values.shape[-1] // 2
    pair_index = jnp.arange(half_dim).astype(jnp.float32)
    frequency = jnp.exp(pair_index * (-2.0 * math.log(rope_base) / values.shape[-1]))
    angles = token_positions[..., None] * frequency
    lower_half = values[..., :half_dim]
    upper_half = values[..., half_dim:]
    cosine = jnp.cos(angles)
    sine = jnp.sin(angles)
    return jnp.concatenate(
        [lower_half * cosine - upper_half * sine, upper_half * cosine + lower_half * sine], axis=-1
    )


def attend(queries, new_key_rows, fresh_value_rows, key_cache, value_cache, live_length):
    step_count, row_count, query_heads, head_dim = queries.shape
    kv_heads = new_key_rows.shape[2]
    group_size = query_heads // kv_heads
    cache_len = key_cache.shape[2]
    block_len = min(cache_len, 2048)
    score_scale = 1.0 / math.sqrt(head_dim)
    grouped_heads = queries.reshape(step_count, row_count, kv_heads, group_size, head_dim)
    grouped_heads = jnp.transpose(grouped_heads, (1, 2, 3, 0, 4)).reshape(
        row_count, kv_heads, group_size * step_count, head_dim
    )
    fresh_keys = jnp.transpose(new_key_rows, (1, 2, 0, 3))
    fresh_values = jnp.transpose(fresh_value_rows, (1, 2, 0, 3))
    fresh_scores = (
        jnp.einsum("rkqd,rkud->rkqu", grouped_heads, fresh_keys, preferred_element_type=jnp.float32)
        * score_scale
    )
    query_step = jnp.arange(group_size * step_count) % step_count
    allowed = jnp.arange(step_count)[None, :] <= query_step[:, None]
    fresh_scores = jnp.where(allowed, fresh_scores, masked_score)
    running_max = jnp.max(fresh_scores, axis=-1)
    weights = jnp.exp(fresh_scores - running_max[..., None])
    running_sum = jnp.sum(weights, axis=-1)
    numerator = jnp.einsum(
        "rkqu,rkud->rkqd",
        weights.astype(jnp.bfloat16),
        fresh_values,
        preferred_element_type=jnp.float32,
    )
    block_count = (jnp.max(live_length) + block_len - 1) // block_len

    def visit(block_index, carry):
        running_max, running_sum, numerator = carry
        key_block = lax.dynamic_slice_in_dim(key_cache, block_index * block_len, block_len, 2)
        value_block = lax.dynamic_slice_in_dim(value_cache, block_index * block_len, block_len, 2)
        scores = (
            jnp.einsum(
                "rkqd,rkcd->rkqc", grouped_heads, key_block, preferred_element_type=jnp.float32
            )
            * score_scale
        )
        places = block_index * block_len + jnp.arange(block_len)
        inside = places[None, :] < live_length[:, None]
        scores = jnp.where(inside[:, None, None, :], scores, masked_score)
        new_max = jnp.maximum(running_max, jnp.max(scores, axis=-1))
        factor = jnp.exp(running_max - new_max)
        weights = jnp.exp(scores - new_max[..., None])
        running_sum = running_sum * factor + jnp.sum(weights, axis=-1)
        numerator = numerator * factor[..., None] + jnp.einsum(
            "rkqc,rkcd->rkqd",
            weights.astype(jnp.bfloat16),
            value_block,
            preferred_element_type=jnp.float32,
        )
        return (new_max, running_sum, numerator)

    running_max, running_sum, numerator = lax.fori_loop(
        0, block_count, visit, (running_max, running_sum, numerator)
    )
    result = numerator / running_sum[..., None]
    result = result.reshape(row_count, kv_heads, group_size, step_count, head_dim)
    result = jnp.transpose(result, (3, 0, 1, 2, 4)).reshape(
        step_count, row_count, query_heads * head_dim
    )
    return result.astype(jnp.bfloat16)


def shards(
    hidden_in,
    norm_gain,
    w_query,
    key_weight_matrix,
    value_weight_matrix,
    bias_query,
    key_bias_vector,
    value_bias_vector,
    w_out,
    key_cache,
    value_cache,
    lengths,
    finished,
):
    step_count, row_count, model_width = hidden_in.shape
    head_dim = key_cache.shape[3]
    kv_heads = key_cache.shape[1]
    query_heads = bias_query.shape[0] // head_dim
    widened = hidden_in.astype(jnp.float32)
    normed = (
        widened
        * lax.rsqrt(jnp.mean(widened * widened, axis=-1, keepdims=True) + norm_eps)
        * norm_gain.astype(jnp.float32)
    )
    normed = normed.astype(jnp.bfloat16)
    flattened = normed.reshape(step_count * row_count, model_width)
    query_part, key_part, value_part = (
        lax.all_to_all(w_query, "tp", split_axis=1, concat_axis=0, tiled=True),
        lax.all_to_all(key_weight_matrix, "tp", split_axis=1, concat_axis=0, tiled=True),
        lax.all_to_all(value_weight_matrix, "tp", split_axis=1, concat_axis=0, tiled=True),
    )
    out_part = lax.all_to_all(w_out, "tp", split_axis=0, concat_axis=1, tiled=True)
    segments = sent_together((query_part, key_part, value_part), "gen", 0, 1)
    first_sum = jnp.dot(flattened, segments[0], preferred_element_type=jnp.float32)
    second_sum = jnp.dot(flattened, segments[1], preferred_element_type=jnp.float32)
    third_sum = jnp.dot(flattened, segments[2], preferred_element_type=jnp.float32)
    queries = first_sum
    new_key_rows = second_sum
    fresh_value_rows = third_sum
    queries = queries + bias_query.astype(jnp.float32)
    new_key_rows = new_key_rows + key_bias_vector.astype(jnp.float32)
    fresh_value_rows = fresh_value_rows + value_bias_vector.astype(jnp.float32)
    token_positions = (lengths[None, :] + jnp.arange(step_count, dtype=jnp.int32)[:, None]).astype(
        jnp.float32
    )[:, :, None]
    rot_query = apply_rotation(
        queries.reshape(step_count, row_count, query_heads, head_dim), token_positions
    ).astype(jnp.bfloat16)
    rotated_key = apply_rotation(
        new_key_rows.reshape(step_count, row_count, kv_heads, head_dim), token_positions
    ).astype(jnp.bfloat16)
    value_rows_new = fresh_value_rows.reshape(step_count, row_count, kv_heads, head_dim).astype(
        jnp.bfloat16
    )
    live_length = jnp.where(finished != 0, 0, lengths)
    attended = attend(rot_query, rotated_key, value_rows_new, key_cache, value_cache, live_length)
    attended_flat = attended.reshape(step_count * row_count, query_heads * head_dim)
    partial_out = jnp.dot(
        attended_flat,
        lax.all_gather(out_part, "gen", axis=1, tiled=True),
        preferred_element_type=jnp.float32,
    )
    projected = of_everyone(partial_out.astype(jnp.bfloat16), "tp").astype(jnp.float32)
    projected = projected.reshape(step_count, row_count, model_width)
    layer_out = jnp.where(finished[None, :, None] != 0, widened, widened + projected)
    return layer_out.astype(jnp.bfloat16)


def solution(mesh):
    placed = (
        P(None, "gen", None),
        P(),
        P(("gen", "tp"), None),
        P(("gen", "tp"), None),
        P(("gen", "tp"), None),
        P("tp"),
        P("tp"),
        P("tp"),
        P(None, ("gen", "tp")),
        P("gen", "tp", None, None),
        P("gen", "tp", None, None),
        P("gen"),
        P("gen"),
    )
    return jax.shard_map(
        shards, mesh=mesh, in_specs=placed, out_specs=P(None, "gen", None), check_vma=False
    )
```

profile of v0, /device:TPU:1, one launch (start us, length us, event | category | flops | bytes accessed | tf_op | source)
XLA Modules:
  0.0 241.7 jit_solution(11346730564790892831)
XLA Ops:
  6.5 0.0 copy-start
  6.5 0.0 copy-start.6
  6.6 1.0 copy-done
  7.5 0.7 copy_bitcast_fusion.3
  8.2 6.4 %all-to-all-start.1 = ((bf16[64,8,128]{2,0,1:T(8,128)(2,1)}), bf16[64,8,128]{2,0,1:T(8,128)(2,1)S(1)}, u32[]{:S(2)}, u32[]{:S(2)}) async-start(bf16[64,8,128]{2,0,1:T(8,128)(2,1)} %copy_bitcast_fusion.3), calls=%async_computation.1 | async-start | bytes 262144 | tf_op jit(solution)/shard_map/all_to_all | solution.py:139
  14.6 1.6 copy_bitcast_fusion.2
  16.1 3.7 %all-to-all-done.1 = bf16[64,8,128]{2,0,1:T(8,128)(2,1)S(1)} async-done(((bf16[64,8,128]{2,0,1:T(8,128)(2,1)}), bf16[64,8,128]{2,0,1:T(8,128)(2,1)S(1)}, u32[]{:S(2)}, u32[]{:S(2)}) %all-to-all-start.1) | async-done | bytes 131104 | tf_op jit(solution)/shard_map/all_to_all | solution.py:139
  19.8 3.4 %all-to-all-start.2 = ((bf16[64,8,128]{2,0,1:T(8,128)(2,1)}), bf16[64,8,128]{2,0,1:T(8,128)(2,1)S(1)}, u32[]{:S(2)}, u32[]{:S(2)}) async-start(bf16[64,8,128]{2,0,1:T(8,128)(2,1)} %copy_bitcast_fusion.2), calls=%async_computation.2 | async-start | bytes 262144 | tf_op jit(solution)/shard_map/all_to_all | solution.py:140
  23.2 0.0 all-gather.3.cloned.1.call-start
  23.2 1.1 copy.94
  24.3 4.1 %all-to-all-done.2 = bf16[64,8,128]{2,0,1:T(8,128)(2,1)S(1)} async-done(((bf16[64,8,128]{2,0,1:T(8,128)(2,1)}), bf16[64,8,128]{2,0,1:T(8,128)(2,1)S(1)}, u32[]{:S(2)}, u32[]{:S(2)}) %all-to-all-start.2) | async-done | bytes 131104 | tf_op jit(solution)/shard_map/all_to_all | solution.py:140
  28.4 9.6 %all_to_all.81 = bf16[64,8,512]{2,0,1:T(8,128)(2,1)S(1)} all-to-all(bf16[64,8,512]{2,0,1:T(8,128)(2,1)S(1)} %bitcast.117), channel_id=1, replica_groups=mesh['gen'=16,'tp'=8] {'tp'}, dimensions={1} | all-to-all | bytes 1048576 | tf_op jit(solution)/shard_map/all_to_all | solution.py:138
  38.0 1.0 pad_maximum_fusion
  39.0 0.0 all-gather.3.cloned.1.call-update
  39.0 0.0 all-gather.5.cloned.1.call-start
  39.1 1.1 copy.93
  40.2 10.3 %all_to_all.82 = bf16[8,512,64]{1,2,0:T(8,128)(2,1)} all-to-all(bf16[8,512,64]{1,2,0:T(8,128)(2,1)S(1)} %bitcast.118), channel_id=1, replica_groups=mesh['gen'=16,'tp'=8] {'tp'}, dimensions={0} | all-to-all | bytes 1048576 | tf_op jit(solution)/shard_map/all_to_all | solution.py:142
  50.4 0.0 all-gather.5.cloned.1.call-update
  50.5 1.3 fusion.59
  52.4 0.7 convert_element_type.97
  53.2 1.2 fusion.34
  54.3 0.2 fusion.36
  54.6 0.1 reshape.254
  54.6 0.0 copy-done.2
  54.6 0.1 add_convert_fusion.1
  54.7 0.1 copy.60
  54.8 0.0 copy-done.5
  54.9 0.1 multiply_cosine_fusion.1
  55.0 79.3 %all-gather.3.cloned.1.call-done = bf16[8192,768]{1,0:T(8,128)(2,1)} async-done(((bf16[512,768]{1,0:T(8,128)(2,1)}), bf16[8192,768]{1,0:T(8,128)(2,1)}) %all-gather.3.cloned.1.call-update) | async-done | bytes 12582928 | tf_op jit(solution)/shard_map/all_gather | solution.py:16
  134.3 4.7 %fusion.21 = f32[8,512]{1,0:T(8,128)S(1)} fusion(bf16[8,8192]{1,0:T(8,128)(2,1)S(1)} %reshape.254, bf16[8192,768]{1,0:T(8,128)(2,1)} %all-gather.3.cloned.1.call-done, f32[512]{0:T(512)S(1)} %convert_element_type.99), kind=kOutput, calls=%fused_computation.31 | convolution fusion | flops 67112960 | bytes 8538112 | tf_op jit(solution)/shard_map/dot_general | solution.py:144
  139.0 0.1 fusion.40
  139.1 0.1 maximum_bitcast_fusion
  139.2 2.0 fusion.24
  141.2 0.1 fusion.61
  141.2 0.1 fusion.47
  141.4 0.2 fusion.62
  141.6 2.0 fusion.31
  143.6 0.2 convolution_bitcast_fusion.1
  143.8 0.1 divide_convert_fusion
  143.9 63.2 %all-gather.5.cloned.1.call-done = bf16[512,8192]{0,1:T(8,128)(2,1)} async-done(((bf16[512,512]{0,1:T(8,128)(2,1)}), bf16[512,8192]{0,1:T(8,128)(2,1)}) %all-gather.5.cloned.1.call-update) | async-done | bytes 8388624 | tf_op jit(solution)/shard_map/all_gather | solution.py:170
  207.1 5.6 %convolution_convert_fusion = bf16[8,8192]{1,0:T(8,128)(2,1)S(1)} fusion(bf16[512,8192]{0,1:T(8,128)(2,1)} %all-gather.5.cloned.1.call-done, bf16[1,8,4,128]{3,2,1,0:T(4,128)(2,1)S(1)} %bitcast.128), kind=kOutput, calls=%fused_computation.22 | convolution fusion | flops 67174400 | bytes 8527872 | tf_op jit(solution)/shard_map/dot_general | solution.py:168
  212.7 1.1 broadcast_in_dim.37
  213.8 4.1 %all-to-all-start.4 = ((bf16[8,8,8192]{2,1,0:T(8,128)(2,1)}), bf16[8,8,8192]{2,1,0:T(8,128)(2,1)S(1)}, u32[]{:S(2)}, u32[]{:S(2)}) async-start(bf16[8,8,8192]{2,1,0:T(8,128)(2,1)} %broadcast_in_dim.37), calls=%async_computation.4 | async-start | bytes 2097152 | tf_op jit(solution)/shard_map/all_to_all | solution.py:22
  217.9 0.0 copy-done.4
  217.9 15.8 %all-to-all-done.4 = bf16[8,8,8192]{2,1,0:T(8,128)(2,1)S(1)} async-done(((bf16[8,8,8192]{2,1,0:T(8,128)(2,1)}), bf16[8,8,8192]{2,1,0:T(8,128)(2,1)S(1)}, u32[]{:S(2)}, u32[]{:S(2)}) %all-to-all-start.4) | async-done | bytes 1048608 | tf_op jit(solution)/shard_map/all_to_all | solution.py:22
  233.7 0.1 convert_reduce_fusion
  233.9 0.2 reshape.261
  234.0 0.9 fusion.37
  (21 shorter events, 0.1 us)
Async XLA Ops:
  6.5 1.0 copy-start
  6.5 48.1 %copy-start.3 = (s32[2]{0:T(128)S(1)}, s32[2]{0:T(128)}, u32[]{:S(2)}) copy-start(s32[2]{0:T(128)} %param.26) | copy-start | bytes 28
  6.5 47.8 %copy-start.1 = (bf16[4,2,8192]{2,1,0:T(2,128)(2,1)S(1)}, bf16[4,2,8192]{2,1,0:T(2,128)(2,1)}, u32[]{:S(2)}) copy-start(bf16[4,2,8192]{2,1,0:T(2,128)(2,1)} %param.15) | copy-start | bytes 393220
  6.5 48.1 %copy-start.2 = (bf16[512]{0:T(512)(128)(2,1)S(1)}, bf16[512]{0:T(512)(128)(2,1)}, u32[]{:S(2)}) copy-start(bf16[512]{0:T(512)(128)(2,1)} %param.20) | copy-start | bytes 3076
  6.5 48.3 %copy-start.5 = (bf16[128]{0:T(256)(128)(2,1)S(1)}, bf16[128]{0:T(256)(128)(2,1)}, u32[]{:S(2)}) copy-start(bf16[128]{0:T(256)(128)(2,1)} %param.21) | copy-start | bytes 772
  6.5 48.3 %copy-start.6 = (bf16[128]{0:T(256)(128)(2,1)S(1)}, bf16[128]{0:T(256)(128)(2,1)}, u32[]{:S(2)}) copy-start(bf16[128]{0:T(256)(128)(2,1)} %param.22) | copy-start | bytes 772
  8.2 11.6 %all-to-all-start.1 = ((bf16[64,8,128]{2,0,1:T(8,128)(2,1)}), bf16[64,8,128]{2,0,1:T(8,128)(2,1)S(1)}, u32[]{:S(2)}, u32[]{:S(2)}) async-start(bf16[64,8,128]{2,0,1:T(8,128)(2,1)} %copy_bitcast_fusion.3), calls=%async_computation.1 | async-start | bytes 262144 | tf_op jit(solution)/shard_map/all_to_all | solution.py:139
  19.8 8.6 %all-to-all-start.2 = ((bf16[64,8,128]{2,0,1:T(8,128)(2,1)}), bf16[64,8,128]{2,0,1:T(8,128)(2,1)S(1)}, u32[]{:S(2)}, u32[]{:S(2)}) async-start(bf16[64,8,128]{2,0,1:T(8,128)(2,1)} %copy_bitcast_fusion.2), calls=%async_computation.2 | async-start | bytes 262144 | tf_op jit(solution)/shard_map/all_to_all | solution.py:140
  23.2 111.1 %all-gather.3.cloned.1.call-start = ((), (), s32[]{:S(2)}) async-start(), calls=%async_computation.5 | async-start | bytes 13369344 | tf_op jit(solution)/shard_map/all_gather | solution.py:16
  39.0 168.1 %all-gather.5.cloned.1.call-start = ((), (), s32[]{:S(2)}) async-start(), calls=%async_computation.6 | async-start | bytes 8912896 | tf_op jit(solution)/shard_map/all_gather | solution.py:170
  143.8 74.1 %copy-start.4 = (s32[2]{0:T(128)S(1)}, s32[2]{0:T(128)}, u32[]{:S(2)}) copy-start(s32[2]{0:T(128)} %param.27) | copy-start | bytes 28
  213.8 20.0 %all-to-all-start.4 = ((bf16[8,8,8192]{2,1,0:T(8,128)(2,1)}), bf16[8,8,8192]{2,1,0:T(8,128)(2,1)S(1)}, u32[]{:S(2)}, u32[]{:S(2)}) async-start(bf16[8,8,8192]{2,1,0:T(8,128)(2,1)} %broadcast_in_dim.37), calls=%async_computation.4 | async-start | bytes 2097152 | tf_op jit(solution)/shard_map/all_to_all | solution.py:22
Sparse Core Ops, SparseCore 0:
  39.1 95.1 all-gather.2
  136.7 70.3 all-gather.4
where the time goes:
time: 243 us; the launch traced here: 242 us
  waiting for transfers between devices  166 us (68%)
  blocking collectives  19.9 us (8%)
  matrix products  14.7 us (6%)
  between operations  14.3 us (6%)
  starting transfers between devices  13.9 us (6%)
  local copies, waits for them, and re-layouts  6.89 us (3%)
  other arithmetic  6.03 us (2%)
    all_gather x1, waiting for transfers between devices, sent_together(): filled = lax.all_gather(both, axis, axis=dim, tiled=True)  79.3 us
    all_gather x1, waiting for transfers between devices, shards(): lax.all_gather(out_part, 'gen', axis=1, tiled=True)  63.2 us
    all_to_all x1, waiting for transfers between devices, from_everyone(): return lax.all_to_all(copies, axis, split_axis=0, concat_axis=0, tiled=True)  15.8 us
    all_to_all x1, blocking collectives, shards(): lax.all_to_all(w_out, 'tp', split_axis=0, concat_axis=1, tiled=True)  10.3 us
    all_to_all x1, blocking collectives, shards(): lax.all_to_all(w_query, 'tp', split_axis=1, concat_axis=0, tiled=True)  9.63 us
    all_to_all x1, starting transfers between devices, shards(): lax.all_to_all(key_weight_matrix, 'tp', split_axis=1, concat_axis=0, tile...  6.36 us
    dot_general x1, matrix products, shards(): jnp.dot(attended_flat, lax.all_gather(out_part, 'gen', axis=1, tiled=True...  5.64 us
  transfers between devices with their start and end apart: 5, of which 5 were waited for; matrix products, arithmetic and copies ran while one was open for 7% of the time, Pallas kernels for 0%

commit v1 on v0

v1 whole, which is shorter than its diff:
```python
import functools
import math

import jax
import jax.numpy as jnp
from jax import lax
from jax.experimental import pallas as pl
from jax.experimental.pallas import tpu as pltpu
from jax.sharding import PartitionSpec as P

NORM_EPS = 1e-06
ROPE_BASE = 1000000.0
MASKED = -1e30
MESH = pl.DeviceIdType.MESH
GEN, TP = 16, 8
TOK = 8
D = 8192
FB = D // GEN
HD = 128
QW = 512
CW = QW + 2 * HD
SLOTS = 16384
CHUNK = 2048
NCH = SLOTS // CHUNK
PIECES = 4
PIECE = SLOTS // PIECES


def peer(g, t):
    return {"gen": g, "tp": t}


def remote(src, dst, send_sem, recv_sem, g, t):
    return pltpu.make_async_remote_copy(
        src_ref=src, dst_ref=dst, send_sem=send_sem, recv_sem=recv_sem,
        device_id=peer(g, t), device_id_type=MESH,
    )


def kernel(
    hid, gain, wq, wk, wv, bias, wo, kc, vc, lens,
    out_ref,
    h_v, gain_v, bias_v, lens_s, hf_v,
    w_stage, w_full, o_stage, o_full, k_v, v_v,
    x_send, x_recv, p_send, p_recv, a_recv, s_v,
    r_send, r_recv, f_send, f_recv, rope_v,
    small_sem, w_sem, wo_sem, kv_sem,
    x_ss, x_rs, ws_ss, w_rs, o_ss, o_rs, p_ss, p_rs, a_ss, a_rs, r_ss, r_rs, f_ss, f_rs,
):
    g = lax.axis_index("gen")
    t = lax.axis_index("tp")
    zl = lax.rem(t, 2)
    ty = lax.div(t, 2)

    def gn(i):
        return lax.rem(g + i, GEN)

    def tn(j):
        return lax.rem(t + j, TP)

    barrier = pltpu.get_barrier_semaphore()
    for i in range(1, GEN):
        pl.semaphore_signal(barrier, inc=1, device_id=peer(gn(i), t), device_id_type=MESH)
    for j in range(1, TP):
        pl.semaphore_signal(barrier, inc=1, device_id=peer(g, tn(j)), device_id_type=MESH)

    smalls = [
        pltpu.make_async_copy(hid, h_v, small_sem.at[0]),
        pltpu.make_async_copy(gain, gain_v, small_sem.at[1]),
        pltpu.make_async_copy(bias, bias_v, small_sem.at[2]),
        pltpu.make_async_copy(lens, lens_s, small_sem.at[3]),
    ]
    for c in smalls:
        c.start()

    def w_copies(j):
        tj = tn(j)
        dst = w_full.at[t] if j == 0 else w_stage.at[j]
        return [
            pltpu.make_async_copy(wq.at[:, pl.ds(tj * QW, QW)], dst.at[:, pl.ds(0, QW)], w_sem.at[j, 0]),
            pltpu.make_async_copy(wk.at[:, pl.ds(tj * HD, HD)], dst.at[:, pl.ds(QW, HD)], w_sem.at[j, 1]),
            pltpu.make_async_copy(wv.at[:, pl.ds(tj * HD, HD)], dst.at[:, pl.ds(QW + HD, HD)], w_sem.at[j, 2]),
        ]

    def wo_copy(j):
        dst = o_full.at[t] if j == 0 else o_stage.at[j]
        return pltpu.make_async_copy(wo.at[:, pl.ds(tn(j) * QW, QW)], dst, wo_sem.at[j])

    for j in range(TP):
        for c in w_copies(j):
            c.start()
    for j in range(TP):
        wo_copy(j).start()

    def kv_copies():
        res = []
        for n, (src, dst) in enumerate(((kc, k_v), (vc, v_v))):
            for i in range(PIECES):
                for r in range(2):
                    res.append(pltpu.make_async_copy(
                        src.at[r, 0, pl.ds(i * PIECE, PIECE), :],
                        dst.at[r, pl.ds(i * PIECE, PIECE), :],
                        kv_sem.at[n, r, i],
                    ))
        return res

    for c in kv_copies():
        c.start()

    smalls[0].wait()
    smalls[1].wait()
    h = jnp.concatenate([h_v[s].astype(jnp.float32) for s in range(4)], axis=0)
    hf_v[...] = h
    scale = lax.rsqrt(jnp.mean(h * h, axis=-1, keepdims=True) + NORM_EPS)
    normed = (h * scale * gain_v[...]).astype(jnp.bfloat16)
    for i in range(GEN):
        x_send[i] = normed[:, i * FB:(i + 1) * FB]
    x_recv[g] = x_send[g]

    pl.semaphore_wait(barrier, GEN - 1 + TP - 1)

    def x_copy(i):
        return remote(x_send.at[gn(i)], x_recv.at[g], x_ss.at[i], x_rs.at[g], gn(i), t)

    def w_send(j):
        return remote(w_stage.at[j], w_full.at[t], ws_ss.at[j], w_rs.at[t], g, tn(j))

    def o_send(j):
        return remote(o_stage.at[j], o_full.at[t], o_ss.at[j], o_rs.at[t], g, tn(j))

    for i in range(1, GEN):
        x_copy(i).start()
    for j in range(1, TP):
        for c in w_copies(j):
            c.wait()
        w_send(j).start()
    for j in range(1, TP):
        wo_copy(j).wait()
        o_send(j).start()
    for c in w_copies(0):
        c.wait()
    wo_copy(0).wait()

    smalls[3].wait()
    smalls[2].wait()
    row = lax.broadcasted_iota(jnp.int32, (TOK, HD), 0)
    lane = lax.broadcasted_iota(jnp.int32, (TOK, HD), 1)
    odd = lax.rem(row, 2) == 1
    len8 = jnp.where(odd, lens_s[1], lens_s[0])
    position = (len8 + lax.div(row, 2)).astype(jnp.float32)
    pair = lax.rem(lane, HD // 2).astype(jnp.float32)
    angles = position * jnp.exp(pair * (-2.0 * math.log(ROPE_BASE) / HD))
    rope_v[0] = jnp.cos(angles)
    rope_v[1] = jnp.where(lane < HD // 2, -1.0, 1.0) * jnp.sin(angles)

    for i in range(1, GEN):
        src = gn(i)
        remote(x_send.at[src], x_recv.at[src], x_ss.at[i], x_rs.at[src], src, t).wait_recv()
    for j in range(1, TP):
        src = tn(j)
        remote(w_stage.at[j], w_full.at[src], ws_ss.at[j], w_rs.at[src], g, src).wait_recv()

    x_all = x_recv[...].reshape(GEN * TOK, FB)
    w_all = w_full[...].reshape(FB, CW)
    part = jnp.dot(x_all, w_all, preferred_element_type=jnp.float32)
    p_send[...] = part.astype(jnp.bfloat16).reshape(GEN, TOK, CW)

    def p_copy(i):
        return remote(p_send.at[gn(i)], p_recv.at[g], p_ss.at[i], p_rs.at[g], gn(i), t)

    for i in range(1, GEN):
        p_copy(i).start()
    p_recv[g] = p_send[g]
    for i in range(1, GEN):
        src = gn(i)
        remote(p_send.at[src], p_recv.at[src], p_ss.at[i], p_rs.at[src], src, t).wait_recv()
    for c in kv_copies():
        c.wait()

    qkv = jnp.sum(p_recv[...].astype(jnp.float32), axis=0) + bias_v[...]
    cosine = rope_v[0]
    sine = rope_v[1]

    def rotated(x):
        return x * cosine + pltpu.roll(x, HD // 2, axis=1) * sine

    q = jnp.concatenate([rotated(qkv[:, n * HD:(n + 1) * HD]) for n in range(4)], axis=0)
    k_new = rotated(qkv[:, QW:QW + HD]).astype(jnp.bfloat16)
    v_new = qkv[:, QW + HD:].astype(jnp.bfloat16)
    qrow = lax.broadcasted_iota(jnp.int32, (4 * TOK, HD), 0)
    q_odd = lax.rem(qrow, 2) == 1
    q_both = jnp.concatenate(
        [jnp.where(q_odd, 0.0, q), jnp.where(q_odd, q, 0.0)], axis=1
    ).astype(jnp.bfloat16)
    q16 = q.astype(jnp.bfloat16)
    nt = (((1,), (1,)), ((), ()))
    qlen = jnp.where(lax.rem(lax.broadcasted_iota(jnp.int32, (4 * TOK, CHUNK), 0), 2) == 1, lens_s[1], lens_s[0])
    places = lax.broadcasted_iota(jnp.int32, (4 * TOK, CHUNK), 1)

    fresh = lax.dot_general(q16, k_new, nt, preferred_element_type=jnp.float32)
    fq = lax.rem(lax.broadcasted_iota(jnp.int32, (4 * TOK, TOK), 0), TOK)
    fk = lax.broadcasted_iota(jnp.int32, (4 * TOK, TOK), 1)
    seen = (lax.rem(fq, 2) == lax.rem(fk, 2)) & (lax.div(fk, 2) <= lax.div(fq, 2))
    fresh = jnp.where(seen, fresh, MASKED)

    def score(c, top):
        at = pl.multiple_of(c * CHUNK, CHUNK)
        keys = jnp.concatenate([k_v[0, pl.ds(at, CHUNK), :], k_v[1, pl.ds(at, CHUNK), :]], axis=1)
        s = lax.dot_general(q_both, keys, nt, preferred_element_type=jnp.float32)
        s = jnp.where(places < qlen - at, s, MASKED)
        s_v[c] = s
        for n in range(CHUNK // HD):
            top = jnp.maximum(top, s[:, n * HD:(n + 1) * HD])
        return top

    top = lax.fori_loop(0, NCH, score, jnp.full((4 * TOK, HD), MASKED, jnp.float32))
    top = jnp.maximum(jnp.max(top, axis=1, keepdims=True), jnp.max(fresh, axis=1, keepdims=True))
    to_exp = 1.0 / math.sqrt(HD)

    def weigh(c, carry):
        total, acc = carry
        at = pl.multiple_of(c * CHUNK, CHUNK)
        w = jnp.exp((s_v[c] - top) * to_exp)
        for n in range(CHUNK // HD):
            total = total + w[:, n * HD:(n + 1) * HD]
        values = jnp.concatenate([v_v[0, pl.ds(at, CHUNK), :], v_v[1, pl.ds(at, CHUNK), :]], axis=1)
        acc = acc + jnp.dot(w.astype(jnp.bfloat16), values, preferred_element_type=jnp.float32)
        return total, acc

    total, acc = lax.fori_loop(
        0, NCH, weigh,
        (jnp.zeros((4 * TOK, HD), jnp.float32), jnp.zeros((4 * TOK, 2 * HD), jnp.float32)),
    )
    fw = jnp.exp((fresh - top) * to_exp)
    denom = jnp.sum(total, axis=1, keepdims=True) + jnp.sum(fw, axis=1, keepdims=True)
    num = jnp.where(q_odd, acc[:, HD:], acc[:, :HD])
    num = num + jnp.dot(fw.astype(jnp.bfloat16), v_new, preferred_element_type=jnp.float32)
    att = num / denom
    a_recv[g] = jnp.concatenate([att[n * TOK:(n + 1) * TOK] for n in range(4)], axis=1).astype(jnp.bfloat16)

    def a_copy(i):
        return remote(a_recv.at[g], a_recv.at[g], a_ss.at[i], a_rs.at[g], gn(i), t)

    for i in range(1, GEN):
        a_copy(i).start()
    for j in range(1, TP):
        src = tn(j)
        remote(o_stage.at[j], o_full.at[src], o_ss.at[j], o_rs.at[src], g, src).wait_recv()
    for i in range(1, GEN):
        src = gn(i)
        remote(a_recv.at[g], a_recv.at[src], a_ss.at[i], a_rs.at[src], src, t).wait_recv()

    a_all = a_recv[...].reshape(GEN * TOK, QW)
    o_all = o_full[...].reshape(QW, QW)
    outp = lax.dot_general(a_all, o_all, nt, preferred_element_type=jnp.float32)
    for z in range(2):
        for y in range(4):
            r_send[2 * y + z] = outp[64 * z:64 * z + 64, HD * y:HD * y + HD].astype(jnp.bfloat16)

    def r_copy(j):
        return remote(r_send.at[tn(j)], r_recv.at[t], r_ss.at[j], r_rs.at[t], g, tn(j))

    for j in range(1, TP):
        r_copy(j).start()
    r_recv[t] = r_send[t]
    for j in range(1, TP):
        src = tn(j)
        remote(r_send.at[src], r_recv.at[src], r_ss.at[j], r_rs.at[src], g, src).wait_recv()
    full = jnp.sum(r_recv[...].astype(jnp.float32), axis=0).astype(jnp.bfloat16)
    f_send[...] = full.reshape(8, TOK, HD)

    def f_copy(n, j):
        return remote(
            f_send.at[n], f_recv.at[g, ty], f_ss.at[n, j], f_rs.at[g, ty], zl * 8 + n, tn(j)
        )

    own_half = lax.div(g, 8)

    def each_send(act):
        for n in range(8):
            for j in range(TP):
                if j == 0:
                    @pl.when(zl * 8 + n != g)
                    def _():
                        act(f_copy(n, j))
                else:
                    act(f_copy(n, j))

    each_send(lambda c: c.start())

    @pl.when(zl == own_half)
    def _():
        f_recv[g, ty] = f_send[lax.rem(g, 8)]

    for gs in range(GEN):
        for ys in range(4):
            def wait_one(gs=gs, ys=ys):
                remote(
                    f_send.at[0], f_recv.at[gs, ys], f_ss.at[0, 0], f_rs.at[gs, ys],
                    gs, ys * 2 + own_half,
                ).wait_recv()

            @pl.when(jnp.logical_not((g == gs) & (t == ys * 2 + own_half)))
            def _():
                wait_one()

    for c in range(GEN * 4):
        cols = slice(c * HD, (c + 1) * HD)
        block = f_recv[c // 4, c % 4].astype(jnp.float32)
        keep = jnp.where(odd, lens_s[3], lens_s[2]) != 0
        mine = hf_v[:, cols]
        hf_v[:, cols] = jnp.where(keep, mine, mine + block)
    for s in range(4):
        out_ref[s] = hf_v[2 * s:2 * s + 2, :].astype(jnp.bfloat16)

    for i in range(1, GEN):
        x_copy(i).wait_send()
        p_copy(i).wait_send()
        a_copy(i).wait_send()
    for j in range(1, TP):
        w_send(j).wait_send()
        o_send(j).wait_send()
        r_copy(j).wait_send()
    each_send(lambda c: c.wait_send())


def shards(
    hidden_in, norm_gain, w_query, key_weight_matrix, value_weight_matrix, bias_query,
    key_bias_vector, value_bias_vector, w_out, key_cache, value_cache, lengths, finished,
):
    gain = norm_gain.astype(jnp.float32).reshape(1, D)
    bias = jnp.concatenate([bias_query, key_bias_vector, value_bias_vector]).astype(jnp.float32).reshape(1, CW)
    info = jnp.concatenate([lengths, finished])
    any_ = pl.BlockSpec(memory_space=pl.ANY)
    bf16, f32 = jnp.bfloat16, jnp.float32
    dma = pltpu.SemaphoreType.DMA
    return pl.pallas_call(
        kernel,
        out_shape=jax.ShapeDtypeStruct((4, 2, D), bf16),
        in_specs=[any_] * 10,
        out_specs=pl.BlockSpec(memory_space=pltpu.VMEM),
        scratch_shapes=[
            pltpu.VMEM((4, 2, D), bf16),
            pltpu.VMEM((1, D), f32),
            pltpu.VMEM((1, CW), f32),
            pltpu.SMEM((4,), jnp.int32),
            pltpu.VMEM((TOK, D), f32),
            pltpu.VMEM((TP, 64, CW), bf16),
            pltpu.VMEM((TP, 64, CW), bf16),
            pltpu.VMEM((TP, 64, QW), bf16),
            pltpu.VMEM((TP, 64, QW), bf16),
            pltpu.VMEM((2, SLOTS, HD), bf16),
            pltpu.VMEM((2, SLOTS, HD), bf16),
            pltpu.VMEM((GEN, TOK, FB), bf16),
            pltpu.VMEM((GEN, TOK, FB), bf16),
            pltpu.VMEM((GEN, TOK, CW), bf16),
            pltpu.VMEM((GEN, TOK, CW), bf16),
            pltpu.VMEM((GEN, TOK, QW), bf16),
            pltpu.VMEM((NCH, 4 * TOK, CHUNK), f32),
            pltpu.VMEM((TP, 64, HD), bf16),
            pltpu.VMEM((TP, 64, HD), bf16),
            pltpu.VMEM((8, TOK, HD), bf16),
            pltpu.VMEM((GEN, 4, TOK, HD), bf16),
            pltpu.VMEM((2, TOK, HD), f32),
            dma((4,)),
            dma((TP, 3)),
            dma((TP,)),
            dma((2, 2, PIECES)),
            dma((GEN,)), dma((GEN,)),
            dma((TP,)), dma((TP,)),
            dma((TP,)), dma((TP,)),
            dma((GEN,)), dma((GEN,)),
            dma((GEN,)), dma((GEN,)),
            dma((TP,)), dma((TP,)),
            dma((8, TP)), dma((GEN, 4)),
        ],
        compiler_params=pltpu.CompilerParams(
            collective_id=0, has_side_effects=True, vmem_limit_bytes=60 * 1024 * 1024
        ),
        name="layer",
    )(
        hidden_in, gain, w_query, key_weight_matrix, value_weight_matrix, bias, w_out.T,
        key_cache, value_cache, info,
    )


def solution(mesh):
    placed = (
        P(None, "gen", None),
        P(),
        P(("gen", "tp"), None),
        P(("gen", "tp"), None),
        P(("gen", "tp"), None),
        P("tp"),
        P("tp"),
        P("tp"),
        P(None, ("gen", "tp")),
        P("gen", "tp", None, None),
        P("gen", "tp", None, None),
        P("gen"),
        P("gen"),
    )
    return jax.shard_map(
        shards, mesh=mesh, in_specs=placed, out_specs=P(None, "gen", None), check_vma=False
    )
```

time: 243 us -> 65.6 us (0.27)
  waiting for transfers between devices: 166 us -> 0 us
  Pallas kernels: 0 us -> 59.2 us
  blocking collectives: 19.9 us -> 0 us
  matrix products: 14.7 us -> 0 us
  between operations: 14.3 us -> 0.01 us
  starting transfers between devices: 13.9 us -> 0 us
  local copies, waits for them, and re-layouts: 6.89 us -> 2.33 us
    all_gather x2 -> x0, waiting for transfers between devices: 142 us -> none  [the longest x1 79.3 us: sent_together(): filled = lax.all_gather(both, axis, axis=dim, tiled=True)]
    pallas_call x0 -> x1, Pallas kernels: none -> 59.2 us  [shards(): pl.pallas_call(kernel, out_shape=jax.ShapeDtypeStruct((4, 2, D), bf16), i...]
    all_to_all x3 -> x0, waiting for transfers between devices: 23.6 us -> none  [the longest x1 15.8 us: from_everyone(): return lax.all_to_all(copies, axis, split_axis=0, concat_axis=0, tiled=True)]
    all_to_all x2 -> x0, blocking collectives: 19.9 us -> none  [the longest x1 10.3 us: shards(): lax.all_to_all(w_out, 'tp', split_axis=0, concat_axis=1, tiled=True)]
    dot_general x6 -> x0, matrix products: 14.7 us -> none  [the longest x1 5.64 us: shards(): jnp.dot(attended_flat, lax.all_gather(out_part, 'gen', axis=1, tiled=True...]
    all_to_all x3 -> x0, starting transfers between devices: 13.8 us -> none  [the longest x1 6.36 us: shards(): lax.all_to_all(key_weight_matrix, 'tp', split_axis=1, concat_axis=0, tile...]
    all_to_all x4 -> x0, local copies, waits for them, and re-layouts: 4.42 us -> none  [the longest x1 1.58 us: shards(): lax.all_to_all(value_weight_matrix, 'tp', split_axis=1, concat_axis=0, ti...]
  transfers between devices with their start and end apart: 5 -> 0, of which waited for: 5 -> 0; matrix products, arithmetic and copies ran while one was open for 7% -> 0% of each run, Pallas kernels for 0% -> 0%
where the time goes in v1:
time: 65.6 us; the launch traced here: 65.4 us
  Pallas kernels  59.2 us (90%)
  other arithmetic  3.92 us (6%)
  local copies, waits for them, and re-layouts  2.33 us (4%)
    pallas_call x1, Pallas kernels, shards(): pl.pallas_call(kernel, out_shape=jax.ShapeDtypeStruct((4, 2, D), bf16), i...  59.2 us
    unnamed x1, local copies, waits for them, and re-layouts  1.65 us
    reshape x1, other arithmetic, shards(): gain = norm_gain.astype(jnp.float32).reshape(1, D)  1.33 us
    concatenate x1, other arithmetic, shards(): info = jnp.concatenate([lengths, finished])  1.32 us

profile of v1, /device:TPU:1, one launch (start us, length us, event | category | flops | bytes accessed | tf_op | source)
XLA Modules:
  0.0 65.4 jit_solution(16590280549491379374)
XLA Ops:
  0.0 1.3 %pad_add_fusion.lens = s32[4]{0:T(128)} fusion(s32[2]{0:T(128)} %param.25, s32[2]{0:T(128)} %param.24), kind=kLoop, calls=%fused_computation.1 | loop fusion | flops 4 | bytes 32 | tf_op jit(solution)/shard_map/concatenate | solution.py:333
  1.3 0.7 %concatenate.19 = bf16[1,512]{1,0:T(2,128)(2,1)S(1)} reshape(bf16[512]{0:T(512)(128)(2,1)} %param.18) | data formatting | bytes 2048 | tf_op jit(solution)/shard_map/concatenate | solution.py:332
  2.0 1.3 %maximum_convert_fusion.bias = f32[1,768]{1,0:T(1,128)} fusion(bf16[1,128]{1,0:T(2,128)(2,1)} %bitcast.6, bf16[1,128]{1,0:T(2,128)(2,1)} %bitcast.7, bf16[1,512]{1,0:T(2,128)(2,1)S(1)} %concatenate.19), kind=kLoop, calls=%fused_computation | loop fusion | flops 4608 | bytes 4608 | tf_op jit(solution)/shard_map/convert_element_type | solution.py:332
  3.3 1.3 %reshape.50 = f32[8192]{0:T(1024)} convert(bf16[8192]{0:T(1024)(128)(2,1)} %param.14) | non-fusion elementwise | flops 8192 | bytes 49152 | tf_op jit(solution)/shard_map/reshape | solution.py:331
  4.6 59.2 %layer.1 = bf16[4,2,8192]{2,1,0:T(2,128)(2,1)} custom-call(bf16[4,2,8192]{2,1,0:T(2,128)(2,1)} %hid.1, f32[1,8192]{1,0:T(1,128)} %bitcast.5, bf16[64,4096]{1,0:T(8,128)(2,1)} %wq.1, bf16[64,1024]{1,0:T(8,128)(2,1)} %wk.1, bf16[64,1024]{1,0:T(8,128)(2,1)} %wv.1, f32[1,768]{1,0:T(1,128)} %maximum_convert_fusion.bias, bf16[64,4096]{1,0:T(8,128)(2,1)} %bitcast.4, ...), custom_call_target="tpu_custom_call" | custom-call | tf_op jit(solution)/shard_map/layer/pallas_call | solution.py:337
  63.8 1.7 %copy.15 = bf16[4,2,8192]{2,1,0:T(2,128)(2,1)} copy(bf16[4,2,8192]{2,1,0:T(2,128)(2,1)} %layer.1) | data formatting | bytes 262144

commit v2 on v1

v2 whole, which is shorter than its diff:
```python
import functools
import math

import jax
import jax.numpy as jnp
from jax import lax
from jax.experimental import pallas as pl
from jax.experimental.pallas import tpu as pltpu
from jax.sharding import PartitionSpec as P

NORM_EPS = 1e-06
ROPE_BASE = 1000000.0
MASKED = -1e30
MESH = pl.DeviceIdType.MESH
GEN, TP = 16, 8
TOK = 8
D = 8192
FB = D // GEN
HD = 128
QW = 512
CW = QW + 2 * HD
SLOTS = 16384
CHUNK = 2048
NCH = SLOTS // CHUNK
PIECES = 4
PIECE = SLOTS // PIECES


def peer(g, t):
    return {"gen": g, "tp": t}


def remote(src, dst, send_sem, recv_sem, g, t):
    return pltpu.make_async_remote_copy(
        src_ref=src, dst_ref=dst, send_sem=send_sem, recv_sem=recv_sem,
        device_id=peer(g, t), device_id_type=MESH,
    )


class Phase:
    def __init__(self):
        self.now = None

    def __call__(self, name):
        if self.now is not None:
            self.now.__exit__(None, None, None)
        self.now = jax.named_scope(name) if name else None
        if name:
            self.now.__enter__()


def kernel(
    hid, gain, wq, wk, wv, bq, bk, bv, wo, kc, vc, lens, fin,
    out_ref,
    h_v, gain_v, bq_v, bk_v, bv_v, lens_s, fin_s, hf_v, m_v,
    wa_stage, wb_stage, wa_full, wb_full, o_stage, o_full, k_v, v_v, kt_v,
    x_send, x_recv, pa_send, pb_send, pa_recv, pb_recv, a_recv, s_v,
    r_send, r_recv, f_send, f_recv, rope_v,
    small_sem, w_sem, wo_sem, kv_sem,
    x_ss, x_rs, wa_ss, wa_rs, wb_ss, wb_rs, o_ss, o_rs, pa_ss, pa_rs, pb_ss, pb_rs,
    a_ss, a_rs, r_ss, r_rs, f_ss, f_rs,
):
    ph = Phase()
    g = lax.axis_index("gen")
    t = lax.axis_index("tp")
    x, zh, core = lax.div(g, 4), lax.rem(lax.div(g, 2), 2), lax.rem(g, 2)
    ty, zl = lax.div(t, 2), lax.rem(t, 2)
    pa = 2 * ty + core
    pb = 2 * x + core

    def gn(i):
        return lax.rem(g + i, GEN)

    def tn(j):
        return lax.rem(t + j, TP)

    def an(j):
        p = lax.rem(pa + j, TP)
        return p, g - core + lax.rem(p, 2), 2 * lax.div(p, 2) + zl

    def bn(j):
        p = lax.rem(pb + j, TP)
        return p, 4 * lax.div(p, 2) + 2 * zh + lax.rem(p, 2), t

    ph("issue")
    barrier = pltpu.get_barrier_semaphore()

    def greet(gg, tt):
        pl.semaphore_signal(barrier, inc=1, device_id=peer(gg, tt), device_id_type=MESH)

    for i in range(1, GEN):
        greet(gn(i), t)
    for j in range(1, TP):
        greet(g, tn(j))
    for k in range(1, 4):
        greet(g - core + (1 - core), lax.rem(t + 2 * k, TP))

    smalls = [
        pltpu.make_async_copy(src, dst, small_sem.at[n])
        for n, (src, dst) in enumerate((
            (hid, h_v), (gain, gain_v), (bq, bq_v), (bk, bk_v), (bv, bv_v), (lens, lens_s), (fin, fin_s),
        ))
    ]
    for c in smalls:
        c.start()

    def wa_copy(j):
        p = lax.rem(pa + j, TP)
        dst = wa_full if j == 0 else wa_stage
        return pltpu.make_async_copy(wq.at[:, pl.ds(p * QW, QW)], dst.at[p], w_sem.at[p, 0])

    def wb_copies(j):
        p = lax.rem(pb + j, TP)
        dst = (wb_full if j == 0 else wb_stage).at[p]
        return [
            pltpu.make_async_copy(src.at[:, pl.ds(p * HD, HD)], dst.at[:, pl.ds(n * HD, HD)], w_sem.at[p, 1 + n])
            for n, src in enumerate((wk, wv))
        ]

    def wo_copy(j):
        dst = o_full.at[t] if j == 0 else o_stage.at[j]
        return pltpu.make_async_copy(wo.at[:, pl.ds(tn(j) * QW, QW)], dst, wo_sem.at[j])

    for j in range(TP):
        wa_copy(j).start()
        for c in wb_copies(j):
            c.start()

    def kv_copy(n, r, i):
        src, dst = ((kc, k_v), (vc, v_v))[n]
        return pltpu.make_async_copy(
            src.at[r, 0, pl.ds(i * PIECE, PIECE), :],
            dst.at[r, pl.ds(i * PIECE, PIECE), :],
            kv_sem.at[n, r, i],
        )

    ph("norm")
    smalls[0].wait()
    smalls[1].wait()
    h = jnp.concatenate([h_v[s].astype(jnp.float32) for s in range(4)], axis=0)
    hf_v[...] = h
    scale = lax.rsqrt(jnp.mean(h * h, axis=-1, keepdims=True) + NORM_EPS)
    normed = h * scale * gain_v[...].astype(jnp.float32).reshape(1, D)
    row = lax.broadcasted_iota(jnp.int32, (TOK, HD), 0)
    lane = lax.broadcasted_iota(jnp.int32, (TOK, HD), 1)
    stays = (lane < 64) == (zl == 0)
    for n in range(8):
        for m in range(4):
            c0 = normed[:, (8 * n + m) * HD:(8 * n + m + 1) * HD]
            c1 = normed[:, (8 * n + 4 + m) * HD:(8 * n + 5 + m) * HD]
            moved = pltpu.roll(jnp.where(zl == 0, c1, c0), 64, axis=1)
            both = jnp.where(stays, jnp.where(zl == 0, c0, c1), moved)
            m_v[n, m] = both
            x_send[n, :, m * HD:(m + 1) * HD] = both.astype(jnp.bfloat16)
    for z in range(2):
        for m in range(4):
            block = m_v[2 * m + z, ty].astype(jnp.bfloat16)
            for n in range(4):
                x_send[2 * n + z, :, FB + m * HD:FB + (m + 1) * HD] = block
    x_recv[g] = x_send[lax.div(g, 2)]

    ph("barrier")
    pl.semaphore_wait(barrier, GEN - 1 + TP - 1 + 3)
    ph("send_xw")

    def x_copy(i):
        return remote(x_send.at[lax.div(gn(i), 2)], x_recv.at[g], x_ss.at[i], x_rs.at[g], gn(i), t)

    def wa_send(j):
        p, gg, tt = an(j)
        return remote(wa_stage.at[p], wa_full.at[pa], wa_ss.at[j], wa_rs.at[pa], gg, tt)

    def wb_send(j):
        p, gg, tt = bn(j)
        return remote(wb_stage.at[p], wb_full.at[pb], wb_ss.at[j], wb_rs.at[pb], gg, tt)

    def o_send(j):
        return remote(o_stage.at[j], o_full.at[t], o_ss.at[j], o_rs.at[t], g, tn(j))

    for i in range(1, GEN):
        x_copy(i).start()
    for j in range(1, TP):
        wa_copy(j).wait()
        wa_send(j).start()
        for c in wb_copies(j):
            c.wait()
        wb_send(j).start()
    wa_copy(0).wait()
    for c in wb_copies(0):
        c.wait()
    for n in range(2):
        for i in range(PIECES):
            for r in range(2):
                kv_copy(n, r, i).start()
    for j in range(TP):
        wo_copy(j).start()

    ph("rope")
    for c in smalls[2:]:
        c.wait()
    odd = lax.rem(row, 2) == 1
    len8 = jnp.where(odd, lens_s[1], lens_s[0])
    position = (len8 + lax.div(row, 2)).astype(jnp.float32)
    pair = lax.rem(lane, HD // 2).astype(jnp.float32)
    angles = position * jnp.exp(pair * (-2.0 * math.log(ROPE_BASE) / HD))
    rope_v[0] = jnp.cos(angles)
    rope_v[1] = jnp.where(lane < HD // 2, -1.0, 1.0) * jnp.sin(angles)

    ph("turn_k")
    nt = (((1,), (1,)), ((), ()))
    er = lax.broadcasted_iota(jnp.int32, (2 * HD, 2 * HD), 0)
    ec = lax.broadcasted_iota(jnp.int32, (2 * HD, 2 * HD), 1)
    eye = jnp.where(er == ec, 1.0, 0.0).astype(jnp.bfloat16)
    per = PIECE // CHUNK
    for i in range(PIECES):
        for r in range(2):
            kv_copy(0, r, i).wait()

        def turn(c, carry):
            at = pl.multiple_of(c * CHUNK, CHUNK)
            keys = jnp.concatenate([k_v[0, pl.ds(at, CHUNK), :], k_v[1, pl.ds(at, CHUNK), :]], axis=1)
            kt_v[c] = lax.dot_general(eye, keys, nt, preferred_element_type=jnp.float32).astype(jnp.bfloat16)
            return carry

        lax.fori_loop(i * per, (i + 1) * per, turn, 0)

    ph("wait_x")
    for i in range(1, GEN):
        src = gn(i)
        remote(x_send.at[0], x_recv.at[src], x_ss.at[i], x_rs.at[src], src, t).wait_recv()
    ph("wait_wa")
    for j in range(1, TP):
        p, gg, tt = an(j)
        remote(wa_stage.at[p], wa_full.at[p], wa_ss.at[j], wa_rs.at[p], gg, tt).wait_recv()
    ph("qkv")
    part = jnp.dot(
        x_recv[:, :, :FB].reshape(GEN * TOK, FB), wa_full[...].reshape(FB, QW),
        preferred_element_type=jnp.float32,
    )
    pa_send[...] = part.astype(jnp.bfloat16).reshape(GEN, TOK, QW)

    slot_a = 4 * x + 2 * zh + zl
    slot_b = 4 * ty + 2 * zh + zl

    def pa_copy(i):
        return remote(pa_send.at[gn(i)], pa_recv.at[slot_a], pa_ss.at[i], pa_rs.at[slot_a], gn(i), pa)

    def pb_copy(i):
        return remote(pb_send.at[gn(i)], pb_recv.at[slot_b], pb_ss.at[i], pb_rs.at[slot_b], gn(i), pb)

    def unless(own, act):
        @pl.when(jnp.logical_not(own))
        def _():
            act()

    own_a = zl == core
    own_b = t == pb
    for i in range(1, GEN):
        pa_copy(i).start()
    unless(own_a, lambda: pa_copy(0).start())

    @pl.when(own_a)
    def _():
        pa_recv[slot_a] = pa_send[g]

    ph("wait_wb")
    for j in range(1, TP):
        p, gg, tt = bn(j)
        remote(wb_stage.at[p], wb_full.at[p], wb_ss.at[j], wb_rs.at[p], gg, tt).wait_recv()
    ph("kvp")
    part = jnp.dot(
        x_recv[:, :, FB:].reshape(GEN * TOK, FB), wb_full[...].reshape(FB, 2 * HD),
        preferred_element_type=jnp.float32,
    )
    pb_send[...] = part.astype(jnp.bfloat16).reshape(GEN, TOK, 2 * HD)
    for i in range(1, GEN):
        pb_copy(i).start()
    unless(own_b, lambda: pb_copy(0).start())

    @pl.when(own_b)
    def _():
        pb_recv[slot_b] = pb_send[g]

    ph("wait_p")

    def pa_wait(i):
        k = lax.rem(slot_a + i, GEN)
        gg = 4 * lax.div(k, 4) + 2 * lax.rem(lax.div(k, 2), 2) + zl
        remote(pa_send.at[0], pa_recv.at[k], pa_ss.at[i], pa_rs.at[k], gg, 2 * ty + lax.rem(k, 2)).wait_recv()

    def pb_wait(i):
        k = lax.rem(slot_b + i, GEN)
        gg = 4 * ty + 2 * lax.rem(lax.div(k, 2), 2) + zl
        remote(
            pb_send.at[0], pb_recv.at[k], pb_ss.at[i], pb_rs.at[k],
            gg, 2 * lax.div(k, 4) + lax.rem(k, 2),
        ).wait_recv()

    for i in range(1, GEN):
        pa_wait(i)
        pb_wait(i)
    unless(own_a, lambda: pa_wait(0))
    unless(own_b, lambda: pb_wait(0))

    ph("wait_kv")
    for j in range(1, TP):
        wo_copy(j).wait()
        o_send(j).start()
    wo_copy(0).wait()
    for i in range(PIECES):
        for r in range(2):
            kv_copy(1, r, i).wait()

    ph("head")
    cosine = rope_v[0]
    sine = rope_v[1]

    def rotated(v):
        return v * cosine + pltpu.roll(v, HD // 2, axis=1) * sine

    qs = jnp.sum(pa_recv[...].astype(jnp.float32), axis=0) + bq_v[...].astype(jnp.float32).reshape(1, QW)
    kvs = jnp.sum(pb_recv[...].astype(jnp.float32), axis=0)
    q = jnp.concatenate([rotated(qs[:, n * HD:(n + 1) * HD]) for n in range(4)], axis=0)
    k_new = rotated(kvs[:, :HD] + bk_v[...].astype(jnp.float32).reshape(1, HD)).astype(jnp.bfloat16)
    v_new = (kvs[:, HD:] + bv_v[...].astype(jnp.float32).reshape(1, HD)).astype(jnp.bfloat16)
    qrow = lax.broadcasted_iota(jnp.int32, (4 * TOK, HD), 0)
    q_odd = lax.rem(qrow, 2) == 1
    q_both = jnp.concatenate(
        [jnp.where(q_odd, 0.0, q), jnp.where(q_odd, q, 0.0)], axis=1
    ).astype(jnp.bfloat16)
    q16 = q.astype(jnp.bfloat16)
    qlen = jnp.where(lax.rem(lax.broadcasted_iota(jnp.int32, (4 * TOK, CHUNK), 0), 2) == 1, lens_s[1], lens_s[0])
    places = lax.broadcasted_iota(jnp.int32, (4 * TOK, CHUNK), 1)

    fresh = lax.dot_general(q16, k_new, nt, preferred_element_type=jnp.float32)
    fq = lax.rem(lax.broadcasted_iota(jnp.int32, (4 * TOK, TOK), 0), TOK)
    fk = lax.broadcasted_iota(jnp.int32, (4 * TOK, TOK), 1)
    seen = (lax.rem(fq, 2) == lax.rem(fk, 2)) & (lax.div(fk, 2) <= lax.div(fq, 2))
    fresh = jnp.where(seen, fresh, MASKED)

    def score(c, top):
        at = pl.multiple_of(c * CHUNK, CHUNK)
        s = jnp.dot(q_both, kt_v[c], preferred_element_type=jnp.float32)
        s = jnp.where(places < qlen - at, s, MASKED)
        s_v[c] = s
        for n in range(CHUNK // HD):
            top = jnp.maximum(top, s[:, n * HD:(n + 1) * HD])
        return top

    ph("score")
    top = lax.fori_loop(0, NCH, score, jnp.full((4 * TOK, HD), MASKED, jnp.float32))
    top = jnp.maximum(jnp.max(top, axis=1, keepdims=True), jnp.max(fresh, axis=1, keepdims=True))
    to_exp = 1.0 / math.sqrt(HD)

    def weigh(c, carry):
        total, acc = carry
        at = pl.multiple_of(c * CHUNK, CHUNK)
        w = jnp.exp((s_v[c] - top) * to_exp)
        for n in range(CHUNK // HD):
            total = total + w[:, n * HD:(n + 1) * HD]
        values = jnp.concatenate([v_v[0, pl.ds(at, CHUNK), :], v_v[1, pl.ds(at, CHUNK), :]], axis=1)
        acc = acc + jnp.dot(w.astype(jnp.bfloat16), values, preferred_element_type=jnp.float32)
        return total, acc

    ph("weigh")
    total, acc = lax.fori_loop(
        0, NCH, weigh,
        (jnp.zeros((4 * TOK, HD), jnp.float32), jnp.zeros((4 * TOK, 2 * HD), jnp.float32)),
    )
    ph("att_end")
    fw = jnp.exp((fresh - top) * to_exp)
    denom = jnp.sum(total, axis=1, keepdims=True) + jnp.sum(fw, axis=1, keepdims=True)
    num = jnp.where(q_odd, acc[:, HD:], acc[:, :HD])
    num = num + jnp.dot(fw.astype(jnp.bfloat16), v_new, preferred_element_type=jnp.float32)
    att = num / denom
    a_recv[g] = jnp.concatenate([att[n * TOK:(n + 1) * TOK] for n in range(4)], axis=1).astype(jnp.bfloat16)

    def a_copy(i):
        return remote(a_recv.at[g], a_recv.at[g], a_ss.at[i], a_rs.at[g], gn(i), t)

    for i in range(1, GEN):
        a_copy(i).start()
    ph("wait_o")
    for j in range(1, TP):
        src = tn(j)
        remote(o_stage.at[j], o_full.at[src], o_ss.at[j], o_rs.at[src], g, src).wait_recv()
    ph("wait_a")
    for i in range(1, GEN):
        src = gn(i)
        remote(a_recv.at[g], a_recv.at[src], a_ss.at[i], a_rs.at[src], src, t).wait_recv()

    ph("outmm")
    a_all = a_recv[...].reshape(GEN * TOK, QW)
    o_all = o_full[...].reshape(QW, QW)
    outp = lax.dot_general(a_all, o_all, nt, preferred_element_type=jnp.float32)
    for z in range(2):
        for y in range(4):
            r_send[2 * y + z] = outp[64 * z:64 * z + 64, HD * y:HD * y + HD].astype(jnp.bfloat16)

    def r_copy(j):
        return remote(r_send.at[tn(j)], r_recv.at[t], r_ss.at[j], r_rs.at[t], g, tn(j))

    for j in range(1, TP):
        r_copy(j).start()
    r_recv[t] = r_send[t]
    ph("wait_r")
    for j in range(1, TP):
        src = tn(j)
        remote(r_send.at[src], r_recv.at[src], r_ss.at[j], r_rs.at[src], g, src).wait_recv()
    ph("fin")
    full = jnp.sum(r_recv[...].astype(jnp.float32), axis=0).astype(jnp.bfloat16)
    f_send[...] = full.reshape(8, TOK, HD)

    def f_copy(n, j):
        return remote(
            f_send.at[n], f_recv.at[g, ty], f_ss.at[n, j], f_rs.at[g, ty], zl * 8 + n, tn(j)
        )

    own_half = lax.div(g, 8)

    def each_send(act):
        for n in range(8):
            for j in range(TP):
                if j == 0:
                    @pl.when(zl * 8 + n != g)
                    def _():
                        act(f_copy(n, j))
                else:
                    act(f_copy(n, j))

    each_send(lambda c: c.start())

    @pl.when(zl == own_half)
    def _():
        f_recv[g, ty] = f_send[lax.rem(g, 8)]

    ph("wait_f")
    for gs in range(GEN):
        for ys in range(4):
            def wait_one(gs=gs, ys=ys):
                remote(
                    f_send.at[0], f_recv.at[gs, ys], f_ss.at[0, 0], f_rs.at[gs, ys],
                    gs, ys * 2 + own_half,
                ).wait_recv()

            @pl.when(jnp.logical_not((g == gs) & (t == ys * 2 + own_half)))
            def _():
                wait_one()

    ph("out")
    for c in range(GEN * 4):
        cols = slice(c * HD, (c + 1) * HD)
        block = f_recv[c // 4, c % 4].astype(jnp.float32)
        keep = jnp.where(odd, fin_s[1], fin_s[0]) != 0
        mine = hf_v[:, cols]
        hf_v[:, cols] = jnp.where(keep, mine, mine + block)
    for s in range(4):
        out_ref[s] = hf_v[2 * s:2 * s + 2, :].astype(jnp.bfloat16)

    ph("wait_sends")
    for i in range(1, GEN):
        x_copy(i).wait_send()
        pa_copy(i).wait_send()
        pb_copy(i).wait_send()
        a_copy(i).wait_send()
    unless(own_a, lambda: pa_copy(0).wait_send())
    unless(own_b, lambda: pb_copy(0).wait_send())
    for j in range(1, TP):
        wa_send(j).wait_send()
        wb_send(j).wait_send()
        o_send(j).wait_send()
        r_copy(j).wait_send()
    each_send(lambda c: c.wait_send())
    ph(None)


def shards(
    hidden_in, norm_gain, w_query, key_weight_matrix, value_weight_matrix, bias_query,
    key_bias_vector, value_bias_vector, w_out, key_cache, value_cache, lengths, finished,
):
    any_ = pl.BlockSpec(memory_space=pl.ANY)
    bf16, f32 = jnp.bfloat16, jnp.float32
    dma = pltpu.SemaphoreType.DMA
    return pl.pallas_call(
        kernel,
        out_shape=jax.ShapeDtypeStruct((4, 2, D), bf16),
        in_specs=[any_] * 13,
        out_specs=pl.BlockSpec(memory_space=pltpu.VMEM),
        scratch_shapes=[
            pltpu.VMEM((4, 2, D), bf16),
            pltpu.VMEM((D,), bf16),
            pltpu.VMEM((QW,), bf16),
            pltpu.VMEM((HD,), bf16),
            pltpu.VMEM((HD,), bf16),
            pltpu.SMEM((2,), jnp.int32),
            pltpu.SMEM((2,), jnp.int32),
            pltpu.VMEM((TOK, D), f32),
            pltpu.VMEM((8, 4, TOK, HD), f32),
            pltpu.VMEM((TP, 64, QW), bf16),
            pltpu.VMEM((TP, 64, 2 * HD), bf16),
            pltpu.VMEM((TP, 64, QW), bf16),
            pltpu.VMEM((TP, 64, 2 * HD), bf16),
            pltpu.VMEM((TP, 64, QW), bf16),
            pltpu.VMEM((TP, 64, QW), bf16),
            pltpu.VMEM((2, SLOTS, HD), bf16),
            pltpu.VMEM((2, SLOTS, HD), bf16),
            pltpu.VMEM((NCH, 2 * HD, CHUNK), bf16),
            pltpu.VMEM((8, TOK, 2 * FB), bf16),
            pltpu.VMEM((GEN, TOK, 2 * FB), bf16),
            pltpu.VMEM((GEN, TOK, QW), bf16),
            pltpu.VMEM((GEN, TOK, 2 * HD), bf16),
            pltpu.VMEM((GEN, TOK, QW), bf16),
            pltpu.VMEM((GEN, TOK, 2 * HD), bf16),
            pltpu.VMEM((GEN, TOK, QW), bf16),
            pltpu.VMEM((NCH, 4 * TOK, CHUNK), f32),
            pltpu.VMEM((TP, 64, HD), bf16),
            pltpu.VMEM((TP, 64, HD), bf16),
            pltpu.VMEM((8, TOK, HD), bf16),
            pltpu.VMEM((GEN, 4, TOK, HD), bf16),
            pltpu.VMEM((2, TOK, HD), f32),
            dma((7,)),
            dma((TP, 3)),
            dma((TP,)),
            dma((2, 2, PIECES)),
            dma((GEN,)), dma((GEN,)),
            dma((TP,)), dma((TP,)),
            dma((TP,)), dma((TP,)),
            dma((TP,)), dma((TP,)),
            dma((GEN,)), dma((GEN,)),
            dma((GEN,)), dma((GEN,)),
            dma((GEN,)), dma((GEN,)),
            dma((TP,)), dma((TP,)),
            dma((8, TP)), dma((GEN, 4)),
        ],
        compiler_params=pltpu.CompilerParams(
            collective_id=0, has_side_effects=True, vmem_limit_bytes=60 * 1024 * 1024
        ),
        name="layer",
    )(
        hidden_in, norm_gain, w_query, key_weight_matrix, value_weight_matrix, bias_query,
        key_bias_vector, value_bias_vector, w_out.T, key_cache, value_cache, lengths, finished,
    )


def solution(mesh):
    placed = (
        P(None, "gen", None),
        P(),
        P(("gen", "tp"), None),
        P(("gen", "tp"), None),
        P(("gen", "tp"), None),
        P("tp"),
        P("tp"),
        P("tp"),
        P(None, ("gen", "tp")),
        P("gen", "tp", None, None),
        P("gen", "tp", None, None),
        P("gen"),
        P("gen"),
    )
    return jax.shard_map(
        shards, mesh=mesh, in_specs=placed, out_specs=P(None, "gen", None), check_vma=False
    )
```

time: 65.6 us -> 50.4 us (0.77)
  Pallas kernels: 59.2 us -> 48.6 us
  other arithmetic: 3.92 us -> 0 us
  local copies, waits for them, and re-layouts: 2.33 us -> 1.65 us
    pallas_call x1, Pallas kernels: 59.2 us -> 48.6 us  [shards(): pl.pallas_call(kernel, out_shape=jax.ShapeDtypeStruct((4, 2, D), bf16), i...]
    reshape x1 -> x0, other arithmetic: 1.33 us -> none  [shards(): gain = norm_gain.astype(jnp.float32).reshape(1, D)]
    concatenate x1 -> x0, other arithmetic: 1.32 us -> none  [shards(): info = jnp.concatenate([lengths, finished])]
    convert_element_type x1 -> x0, other arithmetic: 1.26 us -> none  [shards(): jnp.concatenate([bias_query, key_bias_vector, value_bias_vector])]
    concatenate x1 -> x0, local copies, waits for them, and re-layouts: 0.68 us -> none  [shards(): jnp.concatenate([bias_query, key_bias_vector, value_bias_vector])]
where the time goes in v2:
time: 50.4 us; the launch traced here: 50.2 us
  Pallas kernels  48.6 us (96%)
  local copies, waits for them, and re-layouts  1.65 us (3%)
    pallas_call x1, Pallas kernels, shards(): pl.pallas_call(kernel, out_shape=jax.ShapeDtypeStruct((4, 2, D), bf16), i...  48.6 us
    unnamed x1, local copies, waits for them, and re-layouts  1.65 us

profile of v2, /device:TPU:1, one launch (start us, length us, event | category | flops | bytes accessed | tf_op | source)
XLA Modules:
  0.0 50.2 jit_solution(7652657970118572368)
XLA Ops:
  0.0 48.6 %layer.1 = bf16[4,2,8192]{2,1,0:T(2,128)(2,1)} custom-call(bf16[4,2,8192]{2,1,0:T(2,128)(2,1)} %hid.1, bf16[8192]{0:T(1024)(128)(2,1)} %gain.1, bf16[64,4096]{1,0:T(8,128)(2,1)} %wq.1, bf16[64,1024]{1,0:T(8,128)(2,1)} %wk.1, bf16[64,1024]{1,0:T(8,128)(2,1)} %wv.1, bf16[512]{0:T(512)(128)(2,1)} %bq.1, bf16[128]{0:T(256)(128)(2,1)} %bk.1, bf16[128]{0:T(256)(128)(2,1)} %bv.1, ...), custom_call_target="tpu_custom_call" | custom-call | tf_op jit(solution)/shard_map/layer/pallas_call | solution.py:484
  48.6 1.7 %copy.15 = bf16[4,2,8192]{2,1,0:T(2,128)(2,1)} copy(bf16[4,2,8192]{2,1,0:T(2,128)(2,1)} %layer.1) | data formatting | bytes 262144

commit v3 on v2

--- a/solution.py
+++ b/solution.py
@@ -20,7 +20,7 @@
 QW = 512
 CW = QW + 2 * HD
 SLOTS = 16384
-CHUNK = 2048
+CHUNK = 4096
 NCH = SLOTS // CHUNK
 PIECES = 4
 PIECE = SLOTS // PIECES
@@ -35,6 +35,10 @@
         src_ref=src, dst_ref=dst, send_sem=send_sem, recv_sem=recv_sem,
         device_id=peer(g, t), device_id_type=MESH,
     )
+
+
+def drained(ref, sem):
+    pltpu.make_async_copy(ref, ref, sem).wait()
 
 
 class Phase:
@@ -54,9 +58,9 @@
     out_ref,
     h_v, gain_v, bq_v, bk_v, bv_v, lens_s, fin_s, hf_v, m_v,
     wa_stage, wb_stage, wa_full, wb_full, o_stage, o_full, k_v, v_v, kt_v,
-    x_send, x_recv, pa_send, pb_send, pa_recv, pb_recv, a_recv, s_v,
-    r_send, r_recv, f_send, f_recv, rope_v,
-    small_sem, w_sem, wo_sem, kv_sem,
+    x_send, x_recv, pa_send, pb_send, pa_recv, pb_recv, a_send, a_recv, s_v,
+    o_rows, r_send, r_recv, f_send, f_recv, rope_v,
+    small_sem, w_sem, kv_sem,
     x_ss, x_rs, wa_ss, wa_rs, wb_ss, wb_rs, o_ss, o_rs, pa_ss, pa_rs, pb_ss, pb_rs,
     a_ss, a_rs, r_ss, r_rs, f_ss, f_rs,
 ):
@@ -107,19 +111,20 @@
     def wa_copy(j):
         p = lax.rem(pa + j, TP)
         dst = wa_full if j == 0 else wa_stage
-        return pltpu.make_async_copy(wq.at[:, pl.ds(p * QW, QW)], dst.at[p], w_sem.at[p, 0])
+        return pltpu.make_async_copy(wq.at[:, pl.ds(p * QW, QW)], dst.at[p], w_sem.at[0])
 
     def wb_copies(j):
         p = lax.rem(pb + j, TP)
         dst = (wb_full if j == 0 else wb_stage).at[p]
         return [
-            pltpu.make_async_copy(src.at[:, pl.ds(p * HD, HD)], dst.at[:, pl.ds(n * HD, HD)], w_sem.at[p, 1 + n])
+            pltpu.make_async_copy(src.at[:, pl.ds(p * HD, HD)], dst.at[:, pl.ds(n * HD, HD)], w_sem.at[1])
             for n, src in enumerate((wk, wv))
         ]
 
     def wo_copy(j):
-        dst = o_full.at[t] if j == 0 else o_stage.at[j]
-        return pltpu.make_async_copy(wo.at[:, pl.ds(tn(j) * QW, QW)], dst, wo_sem.at[j])
+        p = lax.rem(pa + j, TP)
+        dst = o_full if j == 0 else o_stage
+        return pltpu.make_async_copy(wo.at[:, pl.ds(p * QW, QW)], dst.at[p], w_sem.at[2])
 
     for j in range(TP):
         wa_copy(j).start()
@@ -131,7 +136,7 @@
         return pltpu.make_async_copy(
             src.at[r, 0, pl.ds(i * PIECE, PIECE), :],
             dst.at[r, pl.ds(i * PIECE, PIECE), :],
-            kv_sem.at[n, r, i],
+            kv_sem.at[i if n == 0 else PIECES],
         )
 
     ph("norm")
@@ -164,30 +169,27 @@
     ph("send_xw")
 
     def x_copy(i):
-        return remote(x_send.at[lax.div(gn(i), 2)], x_recv.at[g], x_ss.at[i], x_rs.at[g], gn(i), t)
+        return remote(x_send.at[lax.div(gn(i), 2)], x_recv.at[g], x_ss, x_rs, gn(i), t)
 
     def wa_send(j):
         p, gg, tt = an(j)
-        return remote(wa_stage.at[p], wa_full.at[pa], wa_ss.at[j], wa_rs.at[pa], gg, tt)
+        return remote(wa_stage.at[p], wa_full.at[pa], wa_ss, wa_rs, gg, tt)
 
     def wb_send(j):
         p, gg, tt = bn(j)
-        return remote(wb_stage.at[p], wb_full.at[pb], wb_ss.at[j], wb_rs.at[pb], gg, tt)
+        return remote(wb_stage.at[p], wb_full.at[pb], wb_ss, wb_rs, gg, tt)
 
     def o_send(j):
-        return remote(o_stage.at[j], o_full.at[t], o_ss.at[j], o_rs.at[t], g, tn(j))
+        p, gg, tt = an(j)
+        return remote(o_stage.at[p], o_full.at[pa], o_ss, o_rs, gg, tt)
 
     for i in range(1, GEN):
         x_copy(i).start()
+    drained(wa_stage, w_sem.at[0])
+    drained(wb_stage, w_sem.at[1])
     for j in range(1, TP):
-        wa_copy(j).wait()
         wa_send(j).start()
-        for c in wb_copies(j):
-            c.wait()
         wb_send(j).start()
-    wa_copy(0).wait()
-    for c in wb_copies(0):
-        c.wait()
     for n in range(2):
         for i in range(PIECES):
             for r in range(2):
@@ -213,8 +215,7 @@
     eye = jnp.where(er == ec, 1.0, 0.0).astype(jnp.bfloat16)
     per = PIECE // CHUNK
     for i in range(PIECES):
-        for r in range(2):
-            kv_copy(0, r, i).wait()
+        drained(k_v.at[:, pl.ds(i * PIECE, PIECE), :], kv_sem.at[i])
 
         def turn(c, carry):
             at = pl.multiple_of(c * CHUNK, CHUNK)
@@ -225,13 +226,9 @@
         lax.fori_loop(i * per, (i + 1) * per, turn, 0)
 
     ph("wait_x")
-    for i in range(1, GEN):
-        src = gn(i)
-        remote(x_send.at[0], x_recv.at[src], x_ss.at[i], x_rs.at[src], src, t).wait_recv()
+    drained(x_recv.at[pl.ds(0, GEN - 1)], x_rs)
     ph("wait_wa")
-    for j in range(1, TP):
-        p, gg, tt = an(j)
-        remote(wa_stage.at[p], wa_full.at[p], wa_ss.at[j], wa_rs.at[p], gg, tt).wait_recv()
+    drained(wa_full.at[pl.ds(0, TP - 1)], wa_rs)
     ph("qkv")
     part = jnp.dot(
         x_recv[:, :, :FB].reshape(GEN * TOK, FB), wa_full[...].reshape(FB, QW),
@@ -243,15 +240,22 @@
     slot_b = 4 * ty + 2 * zh + zl
 
     def pa_copy(i):
-        return remote(pa_send.at[gn(i)], pa_recv.at[slot_a], pa_ss.at[i], pa_rs.at[slot_a], gn(i), pa)
+        return remote(pa_send.at[gn(i)], pa_recv.at[slot_a], pa_ss, pa_rs, gn(i), pa)
 
     def pb_copy(i):
-        return remote(pb_send.at[gn(i)], pb_recv.at[slot_b], pb_ss.at[i], pb_rs.at[slot_b], gn(i), pb)
+        return remote(pb_send.at[gn(i)], pb_recv.at[slot_b], pb_ss, pb_rs, gn(i), pb)
 
     def unless(own, act):
         @pl.when(jnp.logical_not(own))
         def _():
             act()
+
+    def drained_but(own, ref, sem):
+        @pl.when(own)
+        def _():
+            drained(ref.at[pl.ds(0, GEN - 1)], sem)
+
+        unless(own, lambda: drained(ref, sem))
 
     own_a = zl == core
     own_b = t == pb
@@ -264,9 +268,7 @@
         pa_recv[slot_a] = pa_send[g]
 
     ph("wait_wb")
-    for j in range(1, TP):
-        p, gg, tt = bn(j)
-        remote(wb_stage.at[p], wb_full.at[p], wb_ss.at[j], wb_rs.at[p], gg, tt).wait_recv()
+    drained(wb_full.at[pl.ds(0, TP - 1)], wb_rs)
     ph("kvp")
     part = jnp.dot(
         x_recv[:, :, FB:].reshape(GEN * TOK, FB), wb_full[...].reshape(FB, 2 * HD),
@@ -282,34 +284,14 @@
         pb_recv[slot_b] = pb_send[g]
 
     ph("wait_p")
-
-    def pa_wait(i):
-        k = lax.rem(slot_a + i, GEN)
-        gg = 4 * lax.div(k, 4) + 2 * lax.rem(lax.div(k, 2), 2) + zl
-        remote(pa_send.at[0], pa_recv.at[k], pa_ss.at[i], pa_rs.at[k], gg, 2 * ty + lax.rem(k, 2)).wait_recv()
-
-    def pb_wait(i):
-        k = lax.rem(slot_b + i, GEN)
-        gg = 4 * ty + 2 * lax.rem(lax.div(k, 2), 2) + zl
-        remote(
-            pb_send.at[0], pb_recv.at[k], pb_ss.at[i], pb_rs.at[k],
-            gg, 2 * lax.div(k, 4) + lax.rem(k, 2),
-        ).wait_recv()
-
-    for i in range(1, GEN):
-        pa_wait(i)
-        pb_wait(i)
-    unless(own_a, lambda: pa_wait(0))
-    unless(own_b, lambda: pb_wait(0))
-
+    drained_but(own_a, pa_recv, pa_rs)
+    drained_but(own_b, pb_recv, pb_rs)
+    ph("send_o")
+    drained(o_stage, w_sem.at[2])
+    for j in range(1, TP):
+        o_send(j).start()
     ph("wait_kv")
-    for j in range(1, TP):
-        wo_copy(j).wait()
-        o_send(j).start()
-    wo_copy(0).wait()
-    for i in range(PIECES):
-        for r in range(2):
-            kv_copy(1, r, i).wait()
+    drained(v_v, kv_sem.at[PIECES])
 
     ph("head")
     cosine = rope_v[0]
@@ -329,8 +311,8 @@
         [jnp.where(q_odd, 0.0, q), jnp.where(q_odd, q, 0.0)], axis=1
     ).astype(jnp.bfloat16)
     q16 = q.astype(jnp.bfloat16)
-    qlen = jnp.where(lax.rem(lax.broadcasted_iota(jnp.int32, (4 * TOK, CHUNK), 0), 2) == 1, lens_s[1], lens_s[0])
-    places = lax.broadcasted_iota(jnp.int32, (4 * TOK, CHUNK), 1)
+    qlen = jnp.where(q_odd, lens_s[1], lens_s[0])
+    place = lax.broadcasted_iota(jnp.int32, (4 * TOK, HD), 1)
 
     fresh = lax.dot_general(q16, k_new, nt, preferred_element_type=jnp.float32)
     fq = lax.rem(lax.broadcasted_iota(jnp.int32, (4 * TOK, TOK), 0), TOK)
@@ -339,23 +321,23 @@
     fresh = jnp.where(seen, fresh, MASKED)
 
     def score(c, top):
-        at = pl.multiple_of(c * CHUNK, CHUNK)
         s = jnp.dot(q_both, kt_v[c], preferred_element_type=jnp.float32)
-        s = jnp.where(places < qlen - at, s, MASKED)
-        s_v[c] = s
+        rest = qlen - c * CHUNK
         for n in range(CHUNK // HD):
-            top = jnp.maximum(top, s[:, n * HD:(n + 1) * HD])
+            part = jnp.where(place < rest - n * HD, s[:, n * HD:(n + 1) * HD], MASKED)
+            s_v[c, :, n * HD:(n + 1) * HD] = part
+            top = jnp.maximum(top, part)
         return top
 
     ph("score")
     top = lax.fori_loop(0, NCH, score, jnp.full((4 * TOK, HD), MASKED, jnp.float32))
     top = jnp.maximum(jnp.max(top, axis=1, keepdims=True), jnp.max(fresh, axis=1, keepdims=True))
-    to_exp = 1.0 / math.sqrt(HD)
+    to_exp = math.log2(math.e) / math.sqrt(HD)
 
     def weigh(c, carry):
         total, acc = carry
         at = pl.multiple_of(c * CHUNK, CHUNK)
-        w = jnp.exp((s_v[c] - top) * to_exp)
+        w = jnp.exp2((s_v[c] - top) * to_exp)
         for n in range(CHUNK // HD):
             total = total + w[:, n * HD:(n + 1) * HD]
         values = jnp.concatenate([v_v[0, pl.ds(at, CHUNK), :], v_v[1, pl.ds(at, CHUNK), :]], axis=1)
@@ -368,109 +350,99 @@
         (jnp.zeros((4 * TOK, HD), jnp.float32), jnp.zeros((4 * TOK, 2 * HD), jnp.float32)),
     )
     ph("att_end")
-    fw = jnp.exp((fresh - top) * to_exp)
+    fw = jnp.exp2((fresh - top) * to_exp)
     denom = jnp.sum(total, axis=1, keepdims=True) + jnp.sum(fw, axis=1, keepdims=True)
     num = jnp.where(q_odd, acc[:, HD:], acc[:, :HD])
     num = num + jnp.dot(fw.astype(jnp.bfloat16), v_new, preferred_element_type=jnp.float32)
     att = num / denom
-    a_recv[g] = jnp.concatenate([att[n * TOK:(n + 1) * TOK] for n in range(4)], axis=1).astype(jnp.bfloat16)
+    a_send[...] = jnp.concatenate([att[n * TOK:(n + 1) * TOK] for n in range(4)], axis=1).astype(jnp.bfloat16)
 
     def a_copy(i):
-        return remote(a_recv.at[g], a_recv.at[g], a_ss.at[i], a_rs.at[g], gn(i), t)
+        k = lax.rem(slot_a + i, GEN)
+        gg = 4 * lax.div(k, 4) + 2 * lax.rem(lax.div(k, 2), 2) + zl
+        return remote(a_send, a_recv.at[g], a_ss, a_rs, gg, 2 * ty + lax.rem(k, 2))
 
     for i in range(1, GEN):
         a_copy(i).start()
+    unless(own_a, lambda: a_copy(0).start())
+
+    @pl.when(own_a)
+    def _():
+        a_recv[g] = a_send[...]
+
     ph("wait_o")
-    for j in range(1, TP):
-        src = tn(j)
-        remote(o_stage.at[j], o_full.at[src], o_ss.at[j], o_rs.at[src], g, src).wait_recv()
+    drained(o_full.at[pl.ds(0, TP - 1)], o_rs)
     ph("wait_a")
-    for i in range(1, GEN):
-        src = gn(i)
-        remote(a_recv.at[g], a_recv.at[src], a_ss.at[i], a_rs.at[src], src, t).wait_recv()
+    drained_but(own_a, a_recv, a_rs)
 
     ph("outmm")
     a_all = a_recv[...].reshape(GEN * TOK, QW)
     o_all = o_full[...].reshape(QW, QW)
     outp = lax.dot_general(a_all, o_all, nt, preferred_element_type=jnp.float32)
-    for z in range(2):
-        for y in range(4):
-            r_send[2 * y + z] = outp[64 * z:64 * z + 64, HD * y:HD * y + HD].astype(jnp.bfloat16)
+    def group(yy, cc, n):
+        return 4 * lax.rem(x + yy + 2 * n, 4) + 2 * lax.rem(zh + lax.div(yy, 2), 2) + cc
+
+    o_rows[...] = outp.reshape(GEN, TOK, QW)
+    for p in range(TP):
+        for n in range(2):
+            r_send[p, n] = o_rows[group(p // 2, p % 2, n)].astype(jnp.bfloat16)
 
     def r_copy(j):
-        return remote(r_send.at[tn(j)], r_recv.at[t], r_ss.at[j], r_rs.at[t], g, tn(j))
+        p, gg, tt = an(j)
+        return remote(r_send.at[p], r_recv.at[pa], r_ss, r_rs, gg, tt)
 
     for j in range(1, TP):
         r_copy(j).start()
-    r_recv[t] = r_send[t]
+    r_recv[pa] = r_send[pa]
     ph("wait_r")
-    for j in range(1, TP):
-        src = tn(j)
-        remote(r_send.at[src], r_recv.at[src], r_ss.at[j], r_rs.at[src], g, src).wait_recv()
+    drained(r_recv.at[pl.ds(0, TP - 1)], r_rs)
     ph("fin")
     full = jnp.sum(r_recv[...].astype(jnp.float32), axis=0).astype(jnp.bfloat16)
-    f_send[...] = full.reshape(8, TOK, HD)
+    f_send[...] = full
+    slot_f = 4 * x + 2 * zh + zl
+    own_f = ty == 0
 
     def f_copy(n, j):
-        return remote(
-            f_send.at[n], f_recv.at[g, ty], f_ss.at[n, j], f_rs.at[g, ty], zl * 8 + n, tn(j)
-        )
-
-    own_half = lax.div(g, 8)
-
-    def each_send(act):
-        for n in range(8):
-            for j in range(TP):
-                if j == 0:
-                    @pl.when(zl * 8 + n != g)
-                    def _():
-                        act(f_copy(n, j))
-                else:
-                    act(f_copy(n, j))
-
-    each_send(lambda c: c.start())
-
-    @pl.when(zl == own_half)
+        return remote(f_send.at[n], f_recv.at[slot_f], f_ss, f_rs, group(ty, core, n), tn(j))
+
+    for j in range(1, TP):
+        for n in range(2):
+            f_copy(n, j).start()
+    f_copy(1, 0).start()
+    unless(own_f, lambda: f_copy(0, 0).start())
+
+    @pl.when(own_f)
     def _():
-        f_recv[g, ty] = f_send[lax.rem(g, 8)]
+        f_recv[slot_f] = f_send[0]
 
     ph("wait_f")
-    for gs in range(GEN):
-        for ys in range(4):
-            def wait_one(gs=gs, ys=ys):
-                remote(
-                    f_send.at[0], f_recv.at[gs, ys], f_ss.at[0, 0], f_rs.at[gs, ys],
-                    gs, ys * 2 + own_half,
-                ).wait_recv()
-
-            @pl.when(jnp.logical_not((g == gs) & (t == ys * 2 + own_half)))
-            def _():
-                wait_one()
+    drained_but(own_f, f_recv, f_rs)
 
     ph("out")
-    for c in range(GEN * 4):
-        cols = slice(c * HD, (c + 1) * HD)
-        block = f_recv[c // 4, c % 4].astype(jnp.float32)
-        keep = jnp.where(odd, fin_s[1], fin_s[0]) != 0
-        mine = hf_v[:, cols]
-        hf_v[:, cols] = jnp.where(keep, mine, mine + block)
+    keep = jnp.where(odd, fin_s[1], fin_s[0]) != 0
+    first = lane < 64
+    for n in range(8):
+        for m in range(4):
+            z0 = f_recv[2 * n, :, m * HD:(m + 1) * HD].astype(jnp.float32)
+            z1 = f_recv[2 * n + 1, :, m * HD:(m + 1) * HD].astype(jnp.float32)
+            c0 = jnp.where(first, z0, pltpu.roll(z1, 64, axis=1))
+            c1 = jnp.where(first, pltpu.roll(z0, 64, axis=1), z1)
+            for block, c in ((c0, 8 * n + m), (c1, 8 * n + 4 + m)):
+                mine = hf_v[:, c * HD:(c + 1) * HD]
+                hf_v[:, c * HD:(c + 1) * HD] = jnp.where(keep, mine, mine + block)
     for s in range(4):
         out_ref[s] = hf_v[2 * s:2 * s + 2, :].astype(jnp.bfloat16)
 
     ph("wait_sends")
-    for i in range(1, GEN):
-        x_copy(i).wait_send()
-        pa_copy(i).wait_send()
-        pb_copy(i).wait_send()
-        a_copy(i).wait_send()
-    unless(own_a, lambda: pa_copy(0).wait_send())
-    unless(own_b, lambda: pb_copy(0).wait_send())
-    for j in range(1, TP):
-        wa_send(j).wait_send()
-        wb_send(j).wait_send()
-        o_send(j).wait_send()
-        r_copy(j).wait_send()
-    each_send(lambda c: c.wait_send())
+    drained(x_recv.at[pl.ds(0, GEN - 1)], x_ss)
+    drained(wa_full.at[pl.ds(0, TP - 1)], wa_ss)
+    drained(wb_full.at[pl.ds(0, TP - 1)], wb_ss)
+    drained(o_full.at[pl.ds(0, TP - 1)], o_ss)
+    drained_but(own_a, pa_recv, pa_ss)
+    drained_but(own_b, pb_recv, pb_ss)
+    drained_but(own_a, a_recv, a_ss)
+    drained(r_recv.at[pl.ds(0, TP - 1)], r_ss)
+    drained_but(own_f, f_recv, f_ss)
     ph(None)
 
 
@@ -511,27 +483,19 @@
             pltpu.VMEM((GEN, TOK, 2 * HD), bf16),
             pltpu.VMEM((GEN, TOK, QW), bf16),
             pltpu.VMEM((GEN, TOK, 2 * HD), bf16),
+            pltpu.VMEM((TOK, QW), bf16),
             pltpu.VMEM((GEN, TOK, QW), bf16),
             pltpu.VMEM((NCH, 4 * TOK, CHUNK), f32),
-            pltpu.VMEM((TP, 64, HD), bf16),
-            pltpu.VMEM((TP, 64, HD), bf16),
-            pltpu.VMEM((8, TOK, HD), bf16),
-            pltpu.VMEM((GEN, 4, TOK, HD), bf16),
+            pltpu.VMEM((GEN, TOK, QW), f32),
+            pltpu.VMEM((TP, 2, TOK, QW), bf16),
+            pltpu.VMEM((TP, 2, TOK, QW), bf16),
+            pltpu.VMEM((2, TOK, QW), bf16),
+            pltpu.VMEM((GEN, TOK, QW), bf16),
             pltpu.VMEM((2, TOK, HD), f32),
             dma((7,)),
-            dma((TP, 3)),
-            dma((TP,)),
-            dma((2, 2, PIECES)),
-            dma((GEN,)), dma((GEN,)),
-            dma((TP,)), dma((TP,)),
-            dma((TP,)), dma((TP,)),
-            dma((TP,)), dma((TP,)),
-            dma((GEN,)), dma((GEN,)),
-            dma((GEN,)), dma((GEN,)),
-            dma((GEN,)), dma((GEN,)),
-            dma((TP,)), dma((TP,)),
-            dma((8, TP)), dma((GEN, 4)),
-        ],
+            dma((3,)),
+            dma((PIECES + 1,)),
+        ] + [dma(())] * 18,
         compiler_params=pltpu.CompilerParams(
             collective_id=0, has_side_effects=True, vmem_limit_bytes=60 * 1024 * 1024
         ),

time: 50.4 us -> 44.9 us (0.89)
  Pallas kernels: 48.6 us -> 43.1 us
    pallas_call x1, Pallas kernels: 48.6 us -> 43.1 us  [shards(): pl.pallas_call(kernel, out_shape=jax.ShapeDtypeStruct((4, 2, D), bf16), i...]
where the time goes in v3:
time: 44.9 us; the launch traced here: 44.8 us
  Pallas kernels  43.1 us (96%)
  local copies, waits for them, and re-layouts  1.65 us (4%)
    pallas_call x1, Pallas kernels, shards(): pl.pallas_call(kernel, out_shape=jax.ShapeDtypeStruct((4, 2, D), bf16), i...  43.1 us
    unnamed x1, local copies, waits for them, and re-layouts  1.65 us

profile of v3, /device:TPU:1, one launch (start us, length us, event | category | flops | bytes accessed | tf_op | source)
XLA Modules:
  0.0 44.8 jit_solution(1416256482517011641)
XLA Ops:
  0.0 43.1 %layer.1 = bf16[4,2,8192]{2,1,0:T(2,128)(2,1)} custom-call(bf16[4,2,8192]{2,1,0:T(2,128)(2,1)} %hid.1, bf16[8192]{0:T(1024)(128)(2,1)} %gain.1, bf16[64,4096]{1,0:T(8,128)(2,1)} %wq.1, bf16[64,1024]{1,0:T(8,128)(2,1)} %wk.1, bf16[64,1024]{1,0:T(8,128)(2,1)} %wv.1, bf16[512]{0:T(512)(128)(2,1)} %bq.1, bf16[128]{0:T(256)(128)(2,1)} %bk.1, bf16[128]{0:T(256)(128)(2,1)} %bv.1, ...), custom_call_target="tpu_custom_call" | custom-call | tf_op jit(solution)/shard_map/layer/pallas_call | solution.py:456
  43.1 1.7 %copy.15 = bf16[4,2,8192]{2,1,0:T(2,128)(2,1)} copy(bf16[4,2,8192]{2,1,0:T(2,128)(2,1)} %layer.1) | data formatting | bytes 262144

commit v4 on v3

--- a/solution.py
+++ b/solution.py
@@ -20,10 +20,15 @@
 QW = 512
 CW = QW + 2 * HD
 SLOTS = 16384
-CHUNK = 4096
+CHUNK = 8192
 NCH = SLOTS // CHUNK
-PIECES = 4
+PIECES = 2
 PIECE = SLOTS // PIECES
+FAR = sorted(
+    ((dx, dz, d) for dx in range(4) for dz in range(2) for d in (1, 0)),
+    key=lambda o: -(min(o[0], 4 - o[0]) + 2 * o[1]),
+)
+NEAR = [(d, dc) for d in (2, 1, 3, 0) for dc in (1, 0)]
 
 
 def peer(g, t):
@@ -58,10 +63,10 @@
     out_ref,
     h_v, gain_v, bq_v, bk_v, bv_v, lens_s, fin_s, hf_v, m_v,
     wa_stage, wb_stage, wa_full, wb_full, o_stage, o_full, k_v, v_v, kt_v,
-    x_send, x_recv, pa_send, pb_send, pa_recv, pb_recv, a_send, a_recv, s_v,
+    xa_send, xa_recv, xb_send, xb_recv, pa_send, pb_send, pa_recv, pb_recv, a_send, a_recv, s_v, w_v,
     o_rows, r_send, r_recv, f_send, f_recv, rope_v,
     small_sem, w_sem, kv_sem,
-    x_ss, x_rs, wa_ss, wa_rs, wb_ss, wb_rs, o_ss, o_rs, pa_ss, pa_rs, pb_ss, pb_rs,
+    xa_ss, xa_rs, xb_ss, xb_rs, wa_ss, wa_rs, wb_ss, wb_rs, o_ss, o_rs, pa_ss, pa_rs, pb_ss, pb_rs,
     a_ss, a_rs, r_ss, r_rs, f_ss, f_rs,
 ):
     ph = Phase()
@@ -70,66 +75,65 @@
     x, zh, core = lax.div(g, 4), lax.rem(lax.div(g, 2), 2), lax.rem(g, 2)
     ty, zl = lax.div(t, 2), lax.rem(t, 2)
     pa = 2 * ty + core
-    pb = 2 * x + core
-
-    def gn(i):
-        return lax.rem(g + i, GEN)
-
-    def tn(j):
-        return lax.rem(t + j, TP)
-
-    def an(j):
-        p = lax.rem(pa + j, TP)
-        return p, g - core + lax.rem(p, 2), 2 * lax.div(p, 2) + zl
-
-    def bn(j):
-        p = lax.rem(pb + j, TP)
-        return p, 4 * lax.div(p, 2) + 2 * zh + lax.rem(p, 2), t
+    pb = 2 * lax.rem(x + ty, 4) + core
+
+    def gn(dx, dz, dc):
+        return 4 * lax.rem(x + dx, 4) + 2 * lax.rem(zh + dz, 2) + lax.rem(core + dc, 2)
+
+    def an(o):
+        yy, cc = lax.rem(ty + o[0], 4), lax.rem(core + o[1], 2)
+        return 2 * yy + cc, g - core + cc, 2 * yy + zl
+
+    def bn(o):
+        xx, cc = lax.rem(x + o[0], 4), lax.rem(core + o[1], 2)
+        return 2 * lax.rem(xx + ty, 4) + cc, 4 * xx + 2 * zh + cc, t
 
     ph("issue")
-    barrier = pltpu.get_barrier_semaphore()
-
-    def greet(gg, tt):
-        pl.semaphore_signal(barrier, inc=1, device_id=peer(gg, tt), device_id_type=MESH)
-
-    for i in range(1, GEN):
-        greet(gn(i), t)
-    for j in range(1, TP):
-        greet(g, tn(j))
-    for k in range(1, 4):
-        greet(g - core + (1 - core), lax.rem(t + 2 * k, TP))
-
     smalls = [
         pltpu.make_async_copy(src, dst, small_sem.at[n])
         for n, (src, dst) in enumerate((
             (hid, h_v), (gain, gain_v), (bq, bq_v), (bk, bk_v), (bv, bv_v), (lens, lens_s), (fin, fin_s),
         ))
     ]
-    for c in smalls:
+    for c in smalls[:2]:
         c.start()
-
-    def wa_copy(j):
-        p = lax.rem(pa + j, TP)
-        dst = wa_full if j == 0 else wa_stage
+    barrier = pltpu.get_barrier_semaphore()
+
+    def greet(gg, tt):
+        pl.semaphore_signal(barrier, inc=1, device_id=peer(gg, tt), device_id_type=MESH)
+
+    for o in FAR[:-1]:
+        greet(gn(*o), t)
+    for j in range(1, TP):
+        greet(g, lax.rem(t + j, TP))
+    for k in range(1, 4):
+        greet(g - core + (1 - core), lax.rem(t + 2 * k, TP))
+
+    def wa_copy(o):
+        p = an(o)[0]
+        dst = wa_full if o == (0, 0) else wa_stage
         return pltpu.make_async_copy(wq.at[:, pl.ds(p * QW, QW)], dst.at[p], w_sem.at[0])
 
-    def wb_copies(j):
-        p = lax.rem(pb + j, TP)
-        dst = (wb_full if j == 0 else wb_stage).at[p]
+    def wb_copies(o):
+        p = bn(o)[0]
+        slot = 2 * x + core if o == (0, 0) else p
+        dst = (wb_full if o == (0, 0) else wb_stage).at[slot]
         return [
             pltpu.make_async_copy(src.at[:, pl.ds(p * HD, HD)], dst.at[:, pl.ds(n * HD, HD)], w_sem.at[1])
             for n, src in enumerate((wk, wv))
         ]
 
-    def wo_copy(j):
-        p = lax.rem(pa + j, TP)
-        dst = o_full if j == 0 else o_stage
+    def wo_copy(o):
+        p = an(o)[0]
+        dst = o_full if o == (0, 0) else o_stage
         return pltpu.make_async_copy(wo.at[:, pl.ds(p * QW, QW)], dst.at[p], w_sem.at[2])
 
-    for j in range(TP):
-        wa_copy(j).start()
-        for c in wb_copies(j):
+    for o in NEAR:
+        wa_copy(o).start()
+        for c in wb_copies(o):
             c.start()
+    for c in smalls[2:]:
+        c.start()
 
     def kv_copy(n, r, i):
         src, dst = ((kc, k_v), (vc, v_v))[n]
@@ -156,46 +160,53 @@
             moved = pltpu.roll(jnp.where(zl == 0, c1, c0), 64, axis=1)
             both = jnp.where(stays, jnp.where(zl == 0, c0, c1), moved)
             m_v[n, m] = both
-            x_send[n, :, m * HD:(m + 1) * HD] = both.astype(jnp.bfloat16)
+            xa_send[n, :, m * HD:(m + 1) * HD] = both.astype(jnp.bfloat16)
     for z in range(2):
         for m in range(4):
-            block = m_v[2 * m + z, ty].astype(jnp.bfloat16)
-            for n in range(4):
-                x_send[2 * n + z, :, FB + m * HD:FB + (m + 1) * HD] = block
-    x_recv[g] = x_send[lax.div(g, 2)]
+            xb_send[z, :, m * HD:(m + 1) * HD] = m_v[2 * m + z, ty].astype(jnp.bfloat16)
+    xa_recv[g] = xa_send[2 * x + zh]
+    xb_recv[g] = xb_send[zh]
 
     ph("barrier")
     pl.semaphore_wait(barrier, GEN - 1 + TP - 1 + 3)
     ph("send_xw")
 
-    def x_copy(i):
-        return remote(x_send.at[lax.div(gn(i), 2)], x_recv.at[g], x_ss, x_rs, gn(i), t)
-
-    def wa_send(j):
-        p, gg, tt = an(j)
+    def xa_copy(o):
+        gg = gn(*o)
+        return remote(xa_send.at[lax.div(gg, 2)], xa_recv.at[g], xa_ss, xa_rs, gg, t)
+
+    def xb_copy(o):
+        gg = gn(*o)
+        return remote(xb_send.at[lax.rem(lax.div(gg, 2), 2)], xb_recv.at[g], xb_ss, xb_rs, gg, t)
+
+    def wa_send(o):
+        p, gg, tt = an(o)
         return remote(wa_stage.at[p], wa_full.at[pa], wa_ss, wa_rs, gg, tt)
 
-    def wb_send(j):
-        p, gg, tt = bn(j)
-        return remote(wb_stage.at[p], wb_full.at[pb], wb_ss, wb_rs, gg, tt)
-
-    def o_send(j):
-        p, gg, tt = an(j)
+    def wb_send(o):
+        p, gg, tt = bn(o)
+        return remote(wb_stage.at[p], wb_full.at[2 * x + core], wb_ss, wb_rs, gg, tt)
+
+    def o_send(o):
+        p, gg, tt = an(o)
         return remote(o_stage.at[p], o_full.at[pa], o_ss, o_rs, gg, tt)
 
-    for i in range(1, GEN):
-        x_copy(i).start()
     drained(wa_stage, w_sem.at[0])
+    for o in NEAR[:-1]:
+        wa_send(o).start()
+    for o in FAR[:-1]:
+        xa_copy(o).start()
+    for o in FAR[:-1]:
+        xb_copy(o).start()
     drained(wb_stage, w_sem.at[1])
-    for j in range(1, TP):
-        wa_send(j).start()
-        wb_send(j).start()
+    for o in NEAR[:-1]:
+        wb_send(o).start()
     for n in range(2):
         for i in range(PIECES):
             for r in range(2):
                 kv_copy(n, r, i).start()
-    for j in range(TP):
-        wo_copy(j).start()
+    for o in NEAR:
+        wo_copy(o).start()
 
     ph("rope")
     for c in smalls[2:]:
@@ -226,58 +237,60 @@
         lax.fori_loop(i * per, (i + 1) * per, turn, 0)
 
     ph("wait_x")
-    drained(x_recv.at[pl.ds(0, GEN - 1)], x_rs)
+    drained(xa_recv.at[pl.ds(0, GEN - 1)], xa_rs)
+    slot_a = 4 * x + 2 * zh + zl
+    slot_b = 4 * ty + 2 * zh + zl
+    own_a = zl == core
+    own_b = own_a & (x == 0)
+
+    def pa_copy(o):
+        gg = gn(*o)
+        return remote(pa_send.at[gg], pa_recv.at[slot_a], pa_ss, pa_rs, gg, pa)
+
+    def pb_copy(o):
+        gg = gn(*o)
+        return remote(pb_send.at[gg], pb_recv.at[slot_b], pb_ss, pb_rs, gg, pb)
+
+    def unless(own, act):
+        @pl.when(jnp.logical_not(own))
+        def _():
+            act()
+
+    def drained_but(own, ref, sem):
+        @pl.when(own)
+        def _():
+            drained(ref.at[pl.ds(0, GEN - 1)], sem)
+
+        unless(own, lambda: drained(ref, sem))
+
     ph("wait_wa")
     drained(wa_full.at[pl.ds(0, TP - 1)], wa_rs)
     ph("qkv")
     part = jnp.dot(
-        x_recv[:, :, :FB].reshape(GEN * TOK, FB), wa_full[...].reshape(FB, QW),
+        xa_recv[...].reshape(GEN * TOK, FB), wa_full[...].reshape(FB, QW),
         preferred_element_type=jnp.float32,
     )
     pa_send[...] = part.astype(jnp.bfloat16).reshape(GEN, TOK, QW)
-
-    slot_a = 4 * x + 2 * zh + zl
-    slot_b = 4 * ty + 2 * zh + zl
-
-    def pa_copy(i):
-        return remote(pa_send.at[gn(i)], pa_recv.at[slot_a], pa_ss, pa_rs, gn(i), pa)
-
-    def pb_copy(i):
-        return remote(pb_send.at[gn(i)], pb_recv.at[slot_b], pb_ss, pb_rs, gn(i), pb)
-
-    def unless(own, act):
-        @pl.when(jnp.logical_not(own))
-        def _():
-            act()
-
-    def drained_but(own, ref, sem):
-        @pl.when(own)
-        def _():
-            drained(ref.at[pl.ds(0, GEN - 1)], sem)
-
-        unless(own, lambda: drained(ref, sem))
-
-    own_a = zl == core
-    own_b = t == pb
-    for i in range(1, GEN):
-        pa_copy(i).start()
-    unless(own_a, lambda: pa_copy(0).start())
+    for o in FAR[:-1]:
+        pa_copy(o).start()
+    unless(own_a, lambda: pa_copy(FAR[-1]).start())
 
     @pl.when(own_a)
     def _():
         pa_recv[slot_a] = pa_send[g]
 
     ph("wait_wb")
+    drained(xb_recv.at[pl.ds(0, GEN - 1)], xb_rs)
     drained(wb_full.at[pl.ds(0, TP - 1)], wb_rs)
     ph("kvp")
     part = jnp.dot(
-        x_recv[:, :, FB:].reshape(GEN * TOK, FB), wb_full[...].reshape(FB, 2 * HD),
+        xb_recv[...].reshape(GEN * TOK, FB), wb_full[...].reshape(FB, 2 * HD),
         preferred_element_type=jnp.float32,
     )
     pb_send[...] = part.astype(jnp.bfloat16).reshape(GEN, TOK, 2 * HD)
-    for i in range(1, GEN):
-        pb_copy(i).start()
-    unless(own_b, lambda: pb_copy(0).start())
+    for o in FAR[:-1]:
+        pb_copy(o).start()
+    unless(own_b, lambda: pb_copy(FAR[-1]).start())
 
     @pl.when(own_b)
     def _():
@@ -285,13 +298,10 @@
 
     ph("wait_p")
     drained_but(own_a, pa_recv, pa_rs)
-    drained_but(own_b, pb_recv, pb_rs)
     ph("send_o")
     drained(o_stage, w_sem.at[2])
-    for j in range(1, TP):
-        o_send(j).start()
-    ph("wait_kv")
-    drained(v_v, kv_sem.at[PIECES])
+    for o in NEAR[:-1]:
+        o_send(o).start()
 
     ph("head")
     cosine = rope_v[0]
@@ -301,10 +311,7 @@
         return v * cosine + pltpu.roll(v, HD // 2, axis=1) * sine
 
     qs = jnp.sum(pa_recv[...].astype(jnp.float32), axis=0) + bq_v[...].astype(jnp.float32).reshape(1, QW)
-    kvs = jnp.sum(pb_recv[...].astype(jnp.float32), axis=0)
     q = jnp.concatenate([rotated(qs[:, n * HD:(n + 1) * HD]) for n in range(4)], axis=0)
-    k_new = rotated(kvs[:, :HD] + bk_v[...].astype(jnp.float32).reshape(1, HD)).astype(jnp.bfloat16)
-    v_new = (kvs[:, HD:] + bv_v[...].astype(jnp.float32).reshape(1, HD)).astype(jnp.bfloat16)
     qrow = lax.broadcasted_iota(jnp.int32, (4 * TOK, HD), 0)
     q_odd = lax.rem(qrow, 2) == 1
     q_both = jnp.concatenate(
@@ -314,12 +321,6 @@
     qlen = jnp.where(q_odd, lens_s[1], lens_s[0])
     place = lax.broadcasted_iota(jnp.int32, (4 * TOK, HD), 1)
 
-    fresh = lax.dot_general(q16, k_new, nt, preferred_element_type=jnp.float32)
-    fq = lax.rem(lax.broadcasted_iota(jnp.int32, (4 * TOK, TOK), 0), TOK)
-    fk = lax.broadcasted_iota(jnp.int32, (4 * TOK, TOK), 1)
-    seen = (lax.rem(fq, 2) == lax.rem(fk, 2)) & (lax.div(fk, 2) <= lax.div(fq, 2))
-    fresh = jnp.where(seen, fresh, MASKED)
-
     def score(c, top):
         s = jnp.dot(q_both, kt_v[c], preferred_element_type=jnp.float32)
         rest = qlen - c * CHUNK
@@ -331,22 +332,41 @@
 
     ph("score")
     top = lax.fori_loop(0, NCH, score, jnp.full((4 * TOK, HD), MASKED, jnp.float32))
+    ph("wait_pb")
+    drained_but(own_b, pb_recv, pb_rs)
+    drained(v_v, kv_sem.at[PIECES])
+    ph("fresh")
+    kvs = jnp.sum(pb_recv[...].astype(jnp.float32), axis=0)
+    k_new = rotated(kvs[:, :HD] + bk_v[...].astype(jnp.float32).reshape(1, HD)).astype(jnp.bfloat16)
+    v_new = (kvs[:, HD:] + bv_v[...].astype(jnp.float32).reshape(1, HD)).astype(jnp.bfloat16)
+    fresh = lax.dot_general(q16, k_new, nt, preferred_element_type=jnp.float32)
+    fq = lax.rem(lax.broadcasted_iota(jnp.int32, (4 * TOK, TOK), 0), TOK)
+    fk = lax.broadcasted_iota(jnp.int32, (4 * TOK, TOK), 1)
+    seen = (lax.rem(fq, 2) == lax.rem(fk, 2)) & (lax.div(fk, 2) <= lax.div(fq, 2))
+    fresh = jnp.where(seen, fresh, MASKED)
+
     top = jnp.maximum(jnp.max(top, axis=1, keepdims=True), jnp.max(fresh, axis=1, keepdims=True))
     to_exp = math.log2(math.e) / math.sqrt(HD)
 
-    def weigh(c, carry):
-        total, acc = carry
-        at = pl.multiple_of(c * CHUNK, CHUNK)
+    def weights(c, total):
         w = jnp.exp2((s_v[c] - top) * to_exp)
         for n in range(CHUNK // HD):
             total = total + w[:, n * HD:(n + 1) * HD]
+        return w.astype(jnp.bfloat16), total
+
+    def weighed(c, w, acc):
+        at = pl.multiple_of(c * CHUNK, CHUNK)
         values = jnp.concatenate([v_v[0, pl.ds(at, CHUNK), :], v_v[1, pl.ds(at, CHUNK), :]], axis=1)
-        acc = acc + jnp.dot(w.astype(jnp.bfloat16), values, preferred_element_type=jnp.float32)
-        return total, acc
+        return acc + jnp.dot(w, values, preferred_element_type=jnp.float32)
 
     ph("weigh")
+    def step(c, carry):
+        total, acc = carry
+        w, total = weights(c, total)
+        return total, weighed(c, w, acc)
+
     total, acc = lax.fori_loop(
-        0, NCH, weigh,
+        0, NCH, step,
         (jnp.zeros((4 * TOK, HD), jnp.float32), jnp.zeros((4 * TOK, 2 * HD), jnp.float32)),
     )
     ph("att_end")
@@ -357,14 +377,14 @@
     att = num / denom
     a_send[...] = jnp.concatenate([att[n * TOK:(n + 1) * TOK] for n in range(4)], axis=1).astype(jnp.bfloat16)
 
-    def a_copy(i):
-        k = lax.rem(slot_a + i, GEN)
-        gg = 4 * lax.div(k, 4) + 2 * lax.rem(lax.div(k, 2), 2) + zl
-        return remote(a_send, a_recv.at[g], a_ss, a_rs, gg, 2 * ty + lax.rem(k, 2))
-
-    for i in range(1, GEN):
-        a_copy(i).start()
-    unless(own_a, lambda: a_copy(0).start())
+    def a_copy(o):
+        dx, dz, d = o
+        gg = 4 * lax.rem(x + dx, 4) + 2 * lax.rem(zh + dz, 2) + zl
+        return remote(a_send, a_recv.at[g], a_ss, a_rs, gg, 2 * ty + lax.rem(zl + d, 2))
+
+    for o in FAR[:-1]:
+        a_copy(o).start()
+    unless(own_a, lambda: a_copy(FAR[-1]).start())
 
     @pl.when(own_a)
     def _():
@@ -385,31 +405,34 @@
     o_rows[...] = outp.reshape(GEN, TOK, QW)
     for p in range(TP):
         for n in range(2):
-            r_send[p, n] = o_rows[group(p // 2, p % 2, n)].astype(jnp.bfloat16)
-
-    def r_copy(j):
-        p, gg, tt = an(j)
-        return remote(r_send.at[p], r_recv.at[pa], r_ss, r_rs, gg, tt)
-
-    for j in range(1, TP):
-        r_copy(j).start()
-    r_recv[pa] = r_send[pa]
-    ph("wait_r")
-    drained(r_recv.at[pl.ds(0, TP - 1)], r_rs)
-    ph("fin")
-    full = jnp.sum(r_recv[...].astype(jnp.float32), axis=0).astype(jnp.bfloat16)
-    f_send[...] = full
+            r_send[n, p] = o_rows[group(p // 2, p % 2, n)].astype(jnp.bfloat16)
+
+    def r_copy(o, n):
+        p, gg, tt = an(o)
+        return remote(r_send.at[n, p], r_recv.at[n, pa], r_ss, r_rs.at[n], gg, tt)
+
+    for n in (1, 0):
+        for o in NEAR[:-1]:
+            r_copy(o, n).start()
+        r_recv[n, pa] = r_send[n, pa]
     slot_f = 4 * x + 2 * zh + zl
     own_f = ty == 0
 
-    def f_copy(n, j):
-        return remote(f_send.at[n], f_recv.at[slot_f], f_ss, f_rs, group(ty, core, n), tn(j))
-
-    for j in range(1, TP):
-        for n in range(2):
-            f_copy(n, j).start()
-    f_copy(1, 0).start()
-    unless(own_f, lambda: f_copy(0, 0).start())
+    def f_copy(o, n):
+        tt = 2 * lax.rem(ty + o[0], 4) + lax.rem(zl + o[1], 2)
+        return remote(f_send.at[n], f_recv.at[slot_f], f_ss, f_rs, group(ty, core, n), tt)
+
+    for n in (1, 0):
+        ph(f"wait_r{n}")
+        drained(r_recv.at[n, pl.ds(0, TP - 1)], r_rs.at[n])
+        ph(f"fin{n}")
+        f_send[n] = jnp.sum(r_recv[n].astype(jnp.float32), axis=0).astype(jnp.bfloat16)
+        for o in NEAR[:-1]:
+            f_copy(o, n).start()
+        if n == 1:
+            f_copy(NEAR[-1], 1).start()
+        else:
+            unless(own_f, lambda: f_copy(NEAR[-1], 0).start())
 
     @pl.when(own_f)
     def _():
@@ -434,14 +457,15 @@
         out_ref[s] = hf_v[2 * s:2 * s + 2, :].astype(jnp.bfloat16)
 
     ph("wait_sends")
-    drained(x_recv.at[pl.ds(0, GEN - 1)], x_ss)
+    drained(xa_recv.at[pl.ds(0, GEN - 1)], xa_ss)
+    drained(xb_recv.at[pl.ds(0, GEN - 1)], xb_ss)
     drained(wa_full.at[pl.ds(0, TP - 1)], wa_ss)
     drained(wb_full.at[pl.ds(0, TP - 1)], wb_ss)
     drained(o_full.at[pl.ds(0, TP - 1)], o_ss)
     drained_but(own_a, pa_recv, pa_ss)
     drained_but(own_b, pb_recv, pb_ss)
     drained_but(own_a, a_recv, a_ss)
-    drained(r_recv.at[pl.ds(0, TP - 1)], r_ss)
+    drained(r_recv.at[:, pl.ds(0, TP - 1)], r_ss)
     drained_but(own_f, f_recv, f_ss)
     ph(None)
 
@@ -455,7 +479,7 @@
     dma = pltpu.SemaphoreType.DMA
     return pl.pallas_call(
         kernel,
-        out_shape=jax.ShapeDtypeStruct((4, 2, D), bf16),
+        out_shape=pltpu.VMEM((4, 2, D), bf16),
         in_specs=[any_] * 13,
         out_specs=pl.BlockSpec(memory_space=pltpu.VMEM),
         scratch_shapes=[
@@ -477,8 +501,10 @@
             pltpu.VMEM((2, SLOTS, HD), bf16),
             pltpu.VMEM((2, SLOTS, HD), bf16),
             pltpu.VMEM((NCH, 2 * HD, CHUNK), bf16),
-            pltpu.VMEM((8, TOK, 2 * FB), bf16),
-            pltpu.VMEM((GEN, TOK, 2 * FB), bf16),
+            pltpu.VMEM((8, TOK, FB), bf16),
+            pltpu.VMEM((GEN, TOK, FB), bf16),
+            pltpu.VMEM((2, TOK, FB), bf16),
+            pltpu.VMEM((GEN, TOK, FB), bf16),
             pltpu.VMEM((GEN, TOK, QW), bf16),
             pltpu.VMEM((GEN, TOK, 2 * HD), bf16),
             pltpu.VMEM((GEN, TOK, QW), bf16),
@@ -486,16 +512,17 @@
             pltpu.VMEM((TOK, QW), bf16),
             pltpu.VMEM((GEN, TOK, QW), bf16),
             pltpu.VMEM((NCH, 4 * TOK, CHUNK), f32),
+            pltpu.VMEM((2, 4 * TOK, CHUNK), bf16),
             pltpu.VMEM((GEN, TOK, QW), f32),
-            pltpu.VMEM((TP, 2, TOK, QW), bf16),
-            pltpu.VMEM((TP, 2, TOK, QW), bf16),
+            pltpu.VMEM((2, TP, TOK, QW), bf16),
+            pltpu.VMEM((2, TP, TOK, QW), bf16),
             pltpu.VMEM((2, TOK, QW), bf16),
             pltpu.VMEM((GEN, TOK, QW), bf16),
             pltpu.VMEM((2, TOK, HD), f32),
             dma((7,)),
             dma((3,)),
             dma((PIECES + 1,)),
-        ] + [dma(())] * 18,
+        ] + [dma(())] * 17 + [dma((2,))] + [dma(())] * 2,
         compiler_params=pltpu.CompilerParams(
             collective_id=0, has_side_effects=True, vmem_limit_bytes=60 * 1024 * 1024
         ),

time: 44.9 us -> 40.5 us (0.902)
  Pallas kernels: 43.1 us -> 39.7 us
  local copies, waits for them, and re-layouts: 1.65 us -> 0.66 us
    pallas_call x1, Pallas kernels: 43.1 us -> 39.7 us  [shards(): pl.pallas_call(kernel, out_shape=pltpu.VMEM((4, 2, D), bf16), in_specs=[a...]
    unnamed x1, local copies, waits for them, and re-layouts: 1.65 us -> 0.66 us
where the time goes in v4:
time: 40.5 us; the launch traced here: 40.4 us
  Pallas kernels  39.7 us (98%)
  local copies, waits for them, and re-layouts  0.66 us (2%)
    pallas_call x1, Pallas kernels, shards(): pl.pallas_call(kernel, out_shape=pltpu.VMEM((4, 2, D), bf16), in_specs=[a...  39.7 us

profile of v4, /device:TPU:1, one launch (start us, length us, event | category | flops | bytes accessed | tf_op | source)
XLA Modules:
  0.0 40.4 jit_solution(11868502004467728132)
XLA Ops:
  0.0 39.7 %layer.1 = bf16[4,2,8192]{2,1,0:T(2,128)(2,1)S(1)} custom-call(bf16[4,2,8192]{2,1,0:T(2,128)(2,1)} %hid.1, bf16[8192]{0:T(1024)(128)(2,1)} %gain.1, bf16[64,4096]{1,0:T(8,128)(2,1)} %wq.1, bf16[64,1024]{1,0:T(8,128)(2,1)} %wk.1, bf16[64,1024]{1,0:T(8,128)(2,1)} %wv.1, bf16[512]{0:T(512)(128)(2,1)} %bq.1, bf16[128]{0:T(256)(128)(2,1)} %bk.1, ...), custom_call_target="tpu_custom_call" | custom-call | tf_op jit(solution)/shard_map/layer/pallas_call | solution.py:480
  39.7 0.7 %copy.15 = bf16[4,2,8192]{2,1,0:T(2,128)(2,1)} copy(bf16[4,2,8192]{2,1,0:T(2,128)(2,1)S(1)} %layer.1) | data formatting | bytes 262144
